TPU v7x, 32 devices: a whole 2x2x4 slice. The times are simulated.
32 devices in a mesh: seq: 8 (over z, x), tensor: 4 (over y, core).
Axes of the slice: x: 2, y: 2, z: 4, core: 2. Of those that a mesh axis runs over, the one named last changes fastest.
Arguments:
- tokens: bfloat16 [4096, 2048], P('seq', 'tensor'), may hold values from -12 to 12
- attn_gain: float32 [2048], replicated, may hold values from 0.1 to 1.9
- w_query: bfloat16 [2048, 2048], P('seq', 'tensor'), as said below
- w_key: bfloat16 [2048, 512], P('seq', 'tensor'), as said below
- w_value: bfloat16 [2048, 512], P('seq', 'tensor'), may hold values from -0.125 to 0.125
- w_out: bfloat16 [2048, 2048], P('tensor', 'seq'), may hold values from -0.125 to 0.125
- mlp_gain: float32 [2048], replicated, may hold values from 0.1 to 1.9
- w_gate: bfloat16 [2048, 5632], P('seq', 'tensor'), may hold values from -0.125 to 0.125
- w_up: bfloat16 [2048, 5632], P('seq', 'tensor'), may hold values from -0.125 to 0.125
- w_down: bfloat16 [5632, 2048], P('tensor', 'seq'), may hold values from -0.078125 to 0.078125
Outputs:
- layer_out: bfloat16 [4096, 2048], P('seq', 'tensor')
Inputs may be any that keep to these rules, and one draw needn't show every extreme that they name: `w_query`: entries are of order 2048 to the power -1/2. `w_key`: entries are of order 2048 to the power -1/2.
All inputs are finite; a program needn't handle non-finite values.
Results may differ from a plain program's by a relative error of at most 0.013.
Values may be sent and summed in bfloat16 or wider, within the bound.
A program may use at most 128 MiB of HBM per device.

v0:
```python
import functools

import jax
import jax.numpy as jnp
from jax import lax
from jax.experimental import pallas as pl
from jax.experimental.pallas import tpu as pltpu
from jax.sharding import Mesh, PartitionSpec as P

HEAD_DIM = 128
WINDOW = 1024


def product(left, right):
    return jnp.dot(left, right, preferred_element_type=jnp.float32)


def traded(block, cut):
    member = lax.axis_index("pair")
    half = block.shape[cut] // 2
    kept = lax.dynamic_slice_in_dim(block, member * half, half, cut)
    given = lax.dynamic_slice_in_dim(block, (1 - member) * half, half, cut)
    got = lax.ppermute(given, "pair", [(0, 1), (1, 0)])
    first = member == 0
    return jnp.concatenate(
        [jnp.where(first, kept, got), jnp.where(first, got, kept)], axis=1 - cut
    )


def attend(queries, keys, values, first_key):
    rows = queries.shape[0]
    span = keys.shape[0]
    group = queries.shape[1] // HEAD_DIM
    block = queries.reshape(rows, group, HEAD_DIM)
    scores = jnp.einsum("qgd,cd->gqc", block, keys, preferred_element_type=jnp.float32)
    scores = scores * HEAD_DIM ** (-0.5)
    query_pos = lax.broadcasted_iota(jnp.int32, (rows, span), 0)
    key_pos = lax.broadcasted_iota(jnp.int32, (rows, span), 1)
    distance = query_pos + WINDOW - key_pos
    allowed = (distance >= 0) & (distance < WINDOW) & (key_pos + first_key >= 0)
    scores = jnp.where(allowed[None], scores, -1e30)
    highest = jnp.max(scores, axis=2, keepdims=True)
    raised = jnp.exp(scores - highest)
    weights = (raised / jnp.sum(raised, axis=2, keepdims=True)).astype(jnp.bfloat16)
    mixed = jnp.einsum("gqc,cd->qgd", weights, values, preferred_element_type=jnp.float32)
    return mixed.astype(jnp.bfloat16).reshape(rows, group * HEAD_DIM)


def places(chips):
    member, at = lax.axis_index("pair"), lax.axis_index("tensor")
    sibling = at + 1 - 2 * lax.rem(at, 2)

    def ahead(k, start):
        return lax.rem(member + k // chips, 2), lax.rem(start + 2 * (k % chips), 2 * chips)

    def behind(k, start):
        turn = 2 * chips - 2 * (k % chips)
        return lax.rem(member + k // chips, 2), lax.rem(start + turn, 2 * chips)

    return member, at, sibling, ahead, behind


def greet(chips, at, sibling, ahead, member):
    barrier = pltpu.get_barrier_semaphore()
    for k in range(1, 2 * chips):
        there = ahead(k, at)
        pl.semaphore_signal(barrier, inc=1, device_id={"pair": there[0], "tensor": there[1]})
    pl.semaphore_signal(barrier, inc=1, device_id={"pair": member, "tensor": sibling})
    pl.semaphore_wait(barrier, 2 * chips)


def sent(source, target, send, recv, where):
    return pltpu.make_async_remote_copy(
        src_ref=source,
        dst_ref=target,
        send_sem=send,
        recv_sem=recv,
        device_id={"pair": where[0], "tensor": where[1]},
    )


def gather_kernel(chips, x_ref, gain_ref, out_ref, held, own, send, recv, pass_send, pass_recv):
    rows, cols = x_ref.shape
    member, at, sibling, ahead, behind = places(chips)

    def block(where):
        return held.at[
            pl.ds(pl.multiple_of(where[0] * rows, rows), rows),
            pl.ds(pl.multiple_of(where[1] * cols, cols), cols),
        ]

    greet(chips, at, sibling, ahead, member)
    count = 2 * chips
    mine = block((member, at))
    copies = [
        sent(x_ref, mine, send.at[k], recv.at[k], ahead(k, at)) for k in range(1, count)
    ]
    for copy in reversed(copies):
        copy.start()
    passed = [sent(x_ref, mine, pass_send.at[0], pass_recv.at[0], (member, sibling))]
    passed[0].start()
    local = pltpu.make_async_copy(x_ref, mine, own)
    local.start()
    for k in range(1, count):
        came = block(behind(k, at))
        sent(came, came, send.at[k], recv.at[k], (member, sibling)).wait_recv()
        onward = sent(came, came, pass_send.at[k], pass_recv.at[k], (member, sibling))
        onward.start()
        passed.append(onward)
    local.wait()
    for k in range(count):
        came = block(behind(k, sibling))
        sent(came, came, pass_send.at[k], pass_recv.at[k], (member, sibling)).wait_recv()
    for copy in copies + passed:
        copy.wait_send()

    step = 32

    @pl.loop(0, 2 * rows // step)
    def _(index):
        at_rows = pl.ds(pl.multiple_of(index * step, step), step)
        values = held[at_rows, :].astype(jnp.float32)
        mean_square = jnp.mean(values * values, axis=1, keepdims=True)
        scaled = values * lax.rsqrt(mean_square + 1e-06) * gain_ref[...]
        out_ref[at_rows, :] = scaled.astype(out_ref.dtype)


def normed_rows(share, gain, chips, identity):
    rows, cols = share.shape
    count = 2 * chips
    size = (2 * rows, count * cols)
    vmem = pl.BlockSpec(memory_space=pltpu.VMEM)
    return pl.pallas_call(
        functools.partial(gather_kernel, chips),
        out_shape=jax.ShapeDtypeStruct(size, jnp.bfloat16),
        in_specs=[vmem] * 2,
        out_specs=vmem,
        scratch_shapes=[
            pltpu.VMEM(size, jnp.bfloat16),
            pltpu.SemaphoreType.DMA,
            pltpu.SemaphoreType.DMA((count,)),
            pltpu.SemaphoreType.DMA((count,)),
            pltpu.SemaphoreType.DMA((count,)),
            pltpu.SemaphoreType.DMA((count,)),
        ],
        cost_estimate=pl.CostEstimate(
            flops=60 * size[0] * size[1], bytes_accessed=20 * size[0] * size[1], transcendentals=0
        ),
        compiler_params=pltpu.CompilerParams(collective_id=identity, has_side_effects=True),
    )(share, gain.reshape(1, -1))


def sum_kernel(
    chips, terms, base, out_ref, near, stage, far, near_send, near_recv, send, recv
):
    rows, cols = base.shape
    member, at, sibling, ahead, behind = places(chips)
    count = 2 * chips

    def block(where):
        return terms.at[
            pl.ds(pl.multiple_of(where[0] * rows, rows), rows),
            pl.ds(pl.multiple_of(where[1] * cols, cols), cols),
        ]

    greet(chips, at, sibling, ahead, member)
    order = list(range(count - 1, -1, -1))
    given = {
        k: sent(
            block(ahead(k, sibling)),
            near.at[k],
            near_send.at[k],
            near_recv.at[k],
            (member, sibling),
        )
        for k in order
    }
    for k in order:
        given[k].start()
    step = 64
    copies = {}
    for k in order:
        given[k].wait_recv()
        own = block(ahead(k, at))

        @pl.loop(0, rows // step)
        def _(index, k=k, own=own):
            part = pl.ds(pl.multiple_of(index * step, step), step)
            total = own[part, :].astype(jnp.float32) + near[k, part, :].astype(jnp.float32)
            stage[k, part, :] = total.astype(jnp.bfloat16)

        if k:
            copies[k] = sent(stage.at[k], far.at[k], send.at[k], recv.at[k], ahead(k, at))
            copies[k].start()
    for k in order[:-1]:
        copies[k].wait_recv()

    @pl.loop(0, rows // step)
    def _(index):
        part = pl.ds(pl.multiple_of(index * step, step), step)
        total = stage[0, part, :].astype(jnp.float32)
        for k in range(1, count):
            total = total + far[k, part, :].astype(jnp.float32)
        out_ref[part, :] = (base[part, :].astype(jnp.float32) + total).astype(out_ref.dtype)

    for k in order:
        given[k].wait_send()
        if k:
            copies[k].wait_send()


def added_share(terms, base, chips, identity):
    rows, cols = base.shape
    count = 2 * chips
    vmem = pl.BlockSpec(memory_space=pltpu.VMEM)
    slots = pltpu.VMEM((count, rows, cols), jnp.bfloat16)
    return pl.pallas_call(
        functools.partial(sum_kernel, chips),
        out_shape=jax.ShapeDtypeStruct(base.shape, jnp.bfloat16),
        in_specs=[vmem] * 2,
        out_specs=vmem,
        scratch_shapes=[slots] * 3 + [pltpu.SemaphoreType.DMA((count,))] * 4,
        cost_estimate=pl.CostEstimate(
            flops=60 * terms.size, bytes_accessed=20 * terms.size, transcendentals=0
        ),
        compiler_params=pltpu.CompilerParams(collective_id=identity, has_side_effects=True),
    )(terms, base)


def per_device(tokens, attn_gain, w_query, w_key, w_value, w_out, mlp_gain, w_gate, w_up, w_down):
    rows = tokens.shape[0]
    hi, member = lax.axis_index("hi"), lax.axis_index("pair")
    runs = lax.axis_size("hi")
    swap = [(0, 1), (1, 0)]
    first = member == 0
    kept = jnp.where(first, w_key, w_value)
    got = lax.ppermute(jnp.where(first, w_value, w_key), "pair", swap)
    pair_rows = [jnp.where(first, kept, got), jnp.where(first, got, kept)]
    kv_rows = jnp.concatenate(pair_rows, axis=0)
    qkv = jnp.concatenate([traded(w_query, 1), kv_rows], axis=1)
    qkv_full = lax.all_gather(qkv, "hi", axis=0, tiled=True)
    out_full = lax.all_gather(traded(w_out, 0), "hi", axis=1, tiled=True)
    gate_up = jnp.concatenate([traded(w_gate, 1), traded(w_up, 1)], axis=1)
    gate_up_full = lax.all_gather(gate_up, "hi", axis=0, tiled=True)
    down_full = lax.all_gather(traded(w_down, 0), "hi", axis=1, tiled=True)

    chips = lax.axis_size("tensor") // 2
    normed = normed_rows(tokens, attn_gain, chips, 1)
    width = w_query.shape[1] // 2
    projected = product(normed, qkv_full).astype(jnp.bfloat16)
    queries, mine = projected[:, :width], projected[:, width:]
    other = lax.ppermute(mine, "pair", swap)
    onward = [(i, i + 1) for i in range(runs - 1)]
    across = [
        (i * 2 + m, (i + 1) * 2 + 1 - m) for i in range(runs - 1) for m in range(2)
    ]
    mine_before = lax.ppermute(mine, "hi", onward)
    other_before = lax.ppermute(mine, ("hi", "pair"), across)
    mine = jnp.concatenate([mine_before, mine], axis=0)
    other = jnp.concatenate([other_before, other], axis=0)
    keys = jnp.where(first, mine, other)
    values = jnp.where(first, other, mine)
    blocks = []
    before = 2 * rows
    for at in range(0, 2 * rows, rows):
        start = before + at - WINDOW
        stop = before + at + rows
        blocks.append(
            attend(
                queries[at : at + rows],
                keys[start:stop],
                values[start:stop],
                (hi - 1) * before + start,
            )
        )
    attended = jnp.concatenate(blocks, axis=0)
    attn_terms = product(attended, out_full).astype(jnp.bfloat16)
    stream = added_share(attn_terms, tokens, chips, 2)
    stream_normed = normed_rows(stream, mlp_gain, chips, 3)
    units = gate_up_full.shape[1] // 2
    gate_upward = product(stream_normed, gate_up_full)
    gate, upward = gate_upward[:, :units], gate_upward[:, units:]
    hidden = (jax.nn.silu(gate) * upward).astype(jnp.bfloat16)
    return added_share(product(hidden, down_full).astype(jnp.bfloat16), stream, chips, 4)


def solution(mesh):
    sizes = mesh.shape
    split = Mesh(
        mesh.devices.reshape(sizes["seq"] // 2, 2, sizes["tensor"]), ("hi", "pair", "tensor")
    )
    seq = ("hi", "pair")
    in_specs = (
        P(seq, "tensor"),
        P(),
        P(seq, "tensor"),
        P(seq, "tensor"),
        P(seq, "tensor"),
        P("tensor", seq),
        P(),
        P(seq, "tensor"),
        P(seq, "tensor"),
        P("tensor", seq),
    )
    return jax.shard_map(
        per_device, mesh=split, in_specs=in_specs, out_specs=P(seq, "tensor"), check_vma=False
    )
```

profile of v0, /device:TPU:0, one launch (start us, length us, event | category | flops | bytes accessed | tf_op | source)
XLA Modules:
  0.0 311.1 jit_solution(1343620643643725484)
XLA Ops:
  7.6 3.0 collective-permute-start
  12.5 2.1 collective-permute-start.5
  14.5 2.0 collective-permute-done.1
  25.0 9.2 %collective-permute-done.6 = bf16[256,704]{1,0:T(8,128)(2,1)S(1)} collective-permute-done((bf16[256,704]{1,0:T(8,128)(2,1)}, bf16[256,704]{1,0:T(8,128)(2,1)S(1)}, u32[]{:S(2)}, u32[]{:S(2)}) %collective-permute-start.6) | collective-permute-done | bytes 360480 | tf_op jit(solution)/shard_map/ppermute | solution.py:23
  34.5 6.5 %collective-permute-done.7 = bf16[256,704]{1,0:T(8,128)(2,1)S(1)} collective-permute-done((bf16[256,704]{1,0:T(8,128)(2,1)}, bf16[256,704]{1,0:T(8,128)(2,1)S(1)}, u32[]{:S(2)}, u32[]{:S(2)}) %collective-permute-start.7) | collective-permute-done | bytes 360480 | tf_op jit(solution)/shard_map/ppermute | solution.py:23
  42.9 1.8 collective-permute-start.8
  44.7 38.3 %shard_map.100 = bf16[1024,2048]{1,0:T(8,128)(2,1)} custom-call(bf16[512,512]{1,0:T(8,128)(2,1)} %base.1, f32[1,2048]{1,0:T(1,128)} %bitcast.80), custom_call_target="tpu_custom_call" | custom-call | flops 125829120 | bytes 41943040 | tf_op jit(solution)/shard_map/pallas_call | solution.py:133
  85.8 4.5 %convolution_convert_fusion.2 = bf16[1024,384]{0,1:T(8,128)(2,1)S(1)} fusion(bf16[1024,2048]{1,0:T(8,128)(2,1)} %shard_map.100, bf16[2048,384]{1,0:T(8,128)(2,1)} %all-gather.5.cloned.1.call-done), kind=kOutput, calls=%fused_computation.30 | convolution fusion | flops 1611005952 | bytes 6553600 | tf_op jit(solution)/shard_map/dot_general | solution.py:15
  90.3 5.4 %collective-permute-start.2 = (bf16[1024,128]{0,1:T(8,128)(2,1)S(1)}, bf16[1024,128]{0,1:T(8,128)(2,1)}, u32[]{:S(2)}, u32[]{:S(2)}) collective-permute-start(bf16[1024,128]{0,1:T(8,128)(2,1)S(1)} %slice.39), channel_id=1, source_target_pairs={{0,12},{4,8},{8,20},{12,16},{16,28},{20,24},{1,13},{5,9},{9,21},{1... | collective-permute-start | bytes 786440 | tf_op jit(solution)/shard_map/ppermute | solution.py:258
  97.2 3.0 collective-permute-start.4
  101.0 4.7 %collective-permute-done.2 = bf16[1024,128]{0,1:T(8,128)(2,1)} collective-permute-done((bf16[1024,128]{0,1:T(8,128)(2,1)S(1)}, bf16[1024,128]{0,1:T(8,128)(2,1)}, u32[]{:S(2)}, u32[]{:S(2)}) %collective-permute-start.2) | collective-permute-done | bytes 262176 | tf_op jit(solution)/shard_map/ppermute | solution.py:258
  106.8 9.6 %collective-permute-done.4 = bf16[1024,128]{0,1:T(8,128)(2,1)S(1)} collective-permute-done((bf16[1024,128]{0,1:T(8,128)(2,1)S(1)}, bf16[1024,128]{0,1:T(8,128)(2,1)S(1)}, u32[]{:S(2)}, u32[]{:S(2)}) %collective-permute-start.4) | collective-permute-done | bytes 262176 | tf_op jit(solution)/shard_map/ppermute | solution.py:257
  116.7 3.5 %fusion.49 = f32[2,512]{1,0:T(2,128)S(1)} fusion(pred[512,1536]{0,1:T(8,128)(4,1)S(1)} %get-tuple-element.21, bf16[512,2,128]{0,2,1:T(8,128)(2,1)} %bitcast.78, bf16[2048,128]{0,1:T(8,128)(2,1)S(1)} %get-tuple-element.12), kind=kOutput, calls=%fused_computation.88 | convolution fusion | flops 408946176 | bytes 1445888 | tf_op jit(solution)/shard_map/sub | solution.py:43
  120.2 4.2 %fusion.21 = bf16[128,2,512]{2,0,1:T(8,128)(2,1)S(1)} fusion(f32[2,512]{1,0:T(2,128)S(1)} %fusion.49, bf16[2048,128]{0,1:T(8,128)(2,1)S(1)} %get-tuple-element.11, pred[512,1536]{0,1:T(8,128)(4,1)S(1)} %get-tuple-element.21, bf16[512,2,128]{0,2,1:T(8,128)(2,1)} %bitcast.79, bf16[2048,128]{0,1:T(8,128)(2,1)S(1)} %get-tuple-element.12), kind=kOutput, calls=%fused_computation.32 | convolution fusion | flops 813304320 | bytes 2101248 | tf_op jit(solution)/shard_map/gqc,cd->qgd/dot_general | solution.py:45
  124.3 2.5 fusion.48
  126.9 3.2 %fusion.20 = bf16[128,2,512]{2,0,1:T(8,128)(2,1)S(1)} fusion(f32[2,512]{1,0:T(2,128)S(1)} %fusion.48, bf16[2048,128]{0,1:T(8,128)(2,1)S(1)} %get-tuple-element.11, pred[512,1536]{0,1:T(8,128)(4,1)S(1)} %get-tuple-element.22, bf16[512,2,128]{0,2,1:T(8,128)(2,1)S(1)} %bitcast.77, bf16[2048,128]{0,1:T(8,128)(2,1)S(1)} %get-tuple-element.12), kind=kOutput, calls=%fused_computation.31 | convolution fusion | flops 813304320 | bytes 2101248 | tf_op jit(solution)/shard_map/gqc,cd->qgd/dot_general | solution.py:45
  130.1 4.8 %convolution_convert_fusion.1.terms = bf16[1024,2048]{1,0:T(8,128)(2,1)} fusion(bf16[256,2048]{1,0:T(8,128)(2,1)} %all-gather.7.cloned.1.call-done, bf16[512,256]{0,1:T(8,128)(2,1)S(1)} %bitcast.75, bf16[512,256]{0,1:T(8,128)(2,1)S(1)} %bitcast.74), kind=kOutput, calls=%fused_computation.11 | convolution fusion | flops 1076887552 | bytes 5767168 | tf_op jit(solution)/shard_map/dot_general | solution.py:15
  134.8 30.7 %shard_map.101.x_ref.base = bf16[512,512]{1,0:T(8,128)(2,1)} custom-call(bf16[1024,2048]{1,0:T(8,128)(2,1)} %convolution_convert_fusion.1.terms, bf16[512,512]{1,0:T(8,128)(2,1)} %base.1), custom_call_target="tpu_custom_call" | custom-call | flops 125829120 | bytes 41943040 | tf_op jit(solution)/shard_map/pallas_call | solution.py:217
  165.6 36.8 %shard_map.102 = bf16[1024,2048]{1,0:T(8,128)(2,1)} custom-call(bf16[512,512]{1,0:T(8,128)(2,1)} %shard_map.101.x_ref.base, f32[1,2048]{1,0:T(1,128)} %bitcast.81), custom_call_target="tpu_custom_call" | custom-call | flops 125829120 | bytes 41943040 | tf_op jit(solution)/shard_map/pallas_call | solution.py:133
  202.5 11.7 %fusion.50 = f32[1024,1408]{1,0:T(8,128)} fusion(bf16[1024,2048]{1,0:T(8,128)(2,1)} %shard_map.102, bf16[2048,1408]{1,0:T(8,128)(2,1)} %all-gather.9.cloned.1.call-done), kind=kOutput, calls=%fused_computation.89 | convolution fusion | flops 5905580032 | bytes 15728640 | tf_op jit(solution)/shard_map/dot_general | solution.py:15
  214.2 47.5 %all-gather.11.cloned.1.call-done = bf16[704,2048]{1,0:T(8,128)(2,1)} async-done(((bf16[704,512]{1,0:T(8,128)(2,1)}), bf16[704,2048]{1,0:T(8,128)(2,1)}) %all-gather.11.cloned.1.call-update) | async-done | bytes 2883600 | tf_op jit(solution)/shard_map/all_gather | solution.py:245
  261.7 9.1 %convolution_convert_fusion.terms = bf16[1024,2048]{1,0:T(8,128)(2,1)} fusion(bf16[704,2048]{1,0:T(8,128)(2,1)} %all-gather.11.cloned.1.call-done, f32[1024,1408]{1,0:T(8,128)} %fusion.50), kind=kOutput, calls=%fused_computation.10 | convolution fusion | flops 2959212544 | bytes 13369344 | tf_op jit(solution)/shard_map/dot_general | solution.py:15
  270.8 31.9 %shard_map.103 = bf16[512,512]{1,0:T(8,128)(2,1)} custom-call(bf16[1024,2048]{1,0:T(8,128)(2,1)} %convolution_convert_fusion.terms, bf16[512,512]{1,0:T(8,128)(2,1)} %shard_map.101.x_ref.base), custom_call_target="tpu_custom_call" | custom-call | flops 125829120 | bytes 41943040 | tf_op jit(solution)/shard_map/pallas_call | solution.py:217
  302.7 1.9 copy.27
  (51 shorter events, 19.9 us)
Async XLA Ops:
  6.5 14.5 %copy-start = (bf16[256,1408]{1,0:T(8,128)(2,1)S(1)}, bf16[256,1408]{1,0:T(8,128)(2,1)}, u32[]{:S(2)}) copy-start(bf16[256,1408]{1,0:T(8,128)(2,1)} %param.17) | copy-start | bytes 2162692
  6.5 17.2 %copy-start.1 = (bf16[256,1408]{1,0:T(8,128)(2,1)S(1)}, bf16[256,1408]{1,0:T(8,128)(2,1)}, u32[]{:S(2)}) copy-start(bf16[256,1408]{1,0:T(8,128)(2,1)} %param.18) | copy-start | bytes 2162692
  6.5 79.2 %all-gather.5.cloned.1.call-start = ((), (), s32[]{:S(2)}) async-start(), calls=%async_computation | async-start | bytes 1966080 | tf_op jit(solution)/shard_map/all_gather | solution.py:241
  7.6 9.8 %collective-permute-start = (bf16[256,256]{1,0:T(8,128)(2,1)S(1)}, bf16[256,256]{1,0:T(8,128)(2,1)S(1)}, u32[]{:S(2)}, u32[]{:S(2)}) collective-permute-start(bf16[256,256]{1,0:T(8,128)(2,1)S(1)} %constant_dynamic-slice_fusion.4), channel_id=1, source_target_pairs={{0,4},{4,0},{1,5},{5,1},{2,6},{6,2},{3,7},{7,3},{8,12},{12,8},{9,1... | collective-permute-start | bytes 393224 | tf_op jit(solution)/shard_map/ppermute | solution.py:23
  11.5 5.0 %collective-permute-start.1 = (bf16[256,128]{1,0:T(8,128)(2,1)S(1)}, bf16[256,128]{1,0:T(8,128)(2,1)S(1)}, u32[]{:S(2)}, u32[]{:S(2)}) collective-permute-start(bf16[256,128]{1,0:T(8,128)(2,1)S(1)} %broadcast_select_fusion.14), channel_id=1, source_target_pairs={{0,4},{4,0},{1,5},{5,1},{2,6},{6,2},{3,7},{7,3},{8,12},{12,8},{9,1... | collective-permute-start | bytes 196616 | tf_op jit(solution)/shard_map/ppermute | solution.py:237
  12.5 5.8 %collective-permute-start.5 = (bf16[256,256]{1,0:T(8,128)(2,1)S(1)}, bf16[256,256]{1,0:T(8,128)(2,1)S(1)}, u32[]{:S(2)}, u32[]{:S(2)}) collective-permute-start(bf16[256,256]{1,0:T(8,128)(2,1)S(1)} %constant_dynamic-slice_fusion.3), channel_id=1, source_target_pairs={{0,4},{4,0},{1,5},{5,1},{2,6},{6,2},{3,7},{7,3},{8,12},{12,8},{9,1... | collective-permute-start | bytes 393224 | tf_op jit(solution)/shard_map/ppermute | solution.py:23
  20.2 109.9 %all-gather.7.cloned.1.call-start = ((), (), s32[]{:S(2)}) async-start(), calls=%async_computation.1 | async-start | bytes 1310720 | tf_op jit(solution)/shard_map/all_gather | solution.py:242
  21.0 181.5 %all-gather.9.cloned.1.call-start = ((), (), s32[]{:S(2)}) async-start(), calls=%async_computation.2 | async-start | bytes 7208960 | tf_op jit(solution)/shard_map/all_gather | solution.py:244
  22.0 20.8 %copy-start.2 = (bf16[1408,256]{1,0:T(8,128)(2,1)S(1)}, bf16[1408,256]{1,0:T(8,128)(2,1)}, u32[]{:S(2)}) copy-start(bf16[1408,256]{1,0:T(8,128)(2,1)} %param.19) | copy-start | bytes 2162692
  22.0 12.2 %collective-permute-start.6 = (bf16[256,704]{1,0:T(8,128)(2,1)}, bf16[256,704]{1,0:T(8,128)(2,1)S(1)}, u32[]{:S(2)}, u32[]{:S(2)}) collective-permute-start(bf16[256,704]{1,0:T(8,128)(2,1)} %constant_dynamic-slice_fusion.2), channel_id=1, source_target_pairs={{0,4},{4,0},{1,5},{5,1},{2,6},{6,2},{3,7},{7,3},{8,12},{12,8},{9,1... | collective-permute-start | bytes 1081352 | tf_op jit(solution)/shard_map/ppermute | solution.py:23
  24.7 16.2 %collective-permute-start.7 = (bf16[256,704]{1,0:T(8,128)(2,1)}, bf16[256,704]{1,0:T(8,128)(2,1)S(1)}, u32[]{:S(2)}, u32[]{:S(2)}) collective-permute-start(bf16[256,704]{1,0:T(8,128)(2,1)} %constant_dynamic-slice_fusion.1), channel_id=1, source_target_pairs={{0,4},{4,0},{1,5},{5,1},{2,6},{6,2},{3,7},{7,3},{8,12},{12,8},{9,1... | collective-permute-start | bytes 1081352 | tf_op jit(solution)/shard_map/ppermute | solution.py:23
  42.8 218.9 %all-gather.11.cloned.1.call-start = ((), (), s32[]{:S(2)}) async-start(), calls=%async_computation.3 | async-start | bytes 3604480 | tf_op jit(solution)/shard_map/all_gather | solution.py:245
  42.9 41.8 %collective-permute-start.8 = (bf16[704,256]{1,0:T(8,128)(2,1)S(1)}, bf16[704,256]{1,0:T(8,128)(2,1)}, u32[]{:S(2)}, u32[]{:S(2)}) collective-permute-start(bf16[704,256]{1,0:T(8,128)(2,1)S(1)} %constant_dynamic-slice_fusion), channel_id=1, source_target_pairs={{0,4},{4,0},{1,5},{5,1},{2,6},{6,2},{3,7},{7,3},{8,12},{12,8},{9,1... | collective-permute-start | bytes 1081352 | tf_op jit(solution)/shard_map/ppermute | solution.py:23
  90.3 15.5 %collective-permute-start.2 = (bf16[1024,128]{0,1:T(8,128)(2,1)S(1)}, bf16[1024,128]{0,1:T(8,128)(2,1)}, u32[]{:S(2)}, u32[]{:S(2)}) collective-permute-start(bf16[1024,128]{0,1:T(8,128)(2,1)S(1)} %slice.39), channel_id=1, source_target_pairs={{0,12},{4,8},{8,20},{12,16},{16,28},{20,24},{1,13},{5,9},{9,21},{1... | collective-permute-start | bytes 786440 | tf_op jit(solution)/shard_map/ppermute | solution.py:258
  96.6 10.1 %collective-permute-start.3 = (bf16[1024,128]{0,1:T(8,128)(2,1)S(1)}, bf16[1024,128]{0,1:T(8,128)(2,1)S(1)}, u32[]{:S(2)}, u32[]{:S(2)}) collective-permute-start(bf16[1024,128]{0,1:T(8,128)(2,1)S(1)} %slice.39), channel_id=1, source_target_pairs={{0,4},{4,0},{1,5},{5,1},{2,6},{6,2},{3,7},{7,3},{8,12},{12,8},{9,1... | collective-permute-start | bytes 786440 | tf_op jit(solution)/shard_map/ppermute | solution.py:252
  97.2 19.2 %collective-permute-start.4 = (bf16[1024,128]{0,1:T(8,128)(2,1)S(1)}, bf16[1024,128]{0,1:T(8,128)(2,1)S(1)}, u32[]{:S(2)}, u32[]{:S(2)}) collective-permute-start(bf16[1024,128]{0,1:T(8,128)(2,1)S(1)} %slice.39), channel_id=1, source_target_pairs={{0,8},{8,16},{16,24},{1,9},{9,17},{17,25},{2,10},{10,18},{18,26},{... | collective-permute-start | bytes 786440 | tf_op jit(solution)/shard_map/ppermute | solution.py:257
  120.2 4.2 %copy-start.3 = (bf16[512,256]{0,1:T(8,128)(2,1)S(1)}, bf16[512,256]{0,1:T(8,128)(2,1)}, u32[]{:S(2)}) copy-start(bf16[512,256]{0,1:T(8,128)(2,1)} %get-tuple-element.14) | copy-start | bytes 786436
Sparse Core Ops, SparseCore 0:
  20.3 38.5 all-gather.4
  60.4 26.8 all-gather.6
  88.9 111.0 all-gather.8
  201.4 60.2 all-gather.10
where the time goes:
time: 312 us; the launch traced here: 311 us
  Pallas kernels  138 us (44%)
  waiting for transfers between devices  80.6 us (26%)
  matrix products  43.5 us (14%)
  starting transfers between devices  18.1 us (6%)
  between operations  13.4 us (4%)
  other arithmetic  10.2 us (3%)
  local copies, waits for them, and re-layouts  7.57 us (2%)
    pallas_call x2, Pallas kernels, normed_rows(): pl.pallas_call(functools.partial(gather_kernel, chips), out_shape=jax.Sha...  75.1 us
    pallas_call x2, Pallas kernels, added_share(): pl.pallas_call(functools.partial(sum_kernel, chips), out_shape=jax.ShapeD...  62.6 us
    all_gather x1, waiting for transfers between devices, per_device(): down_full = lax.all_gather(traded(w_down, 0), 'hi', axis=1, tiled=True)  47.5 us
    dot_general x4, matrix products, product(): return jnp.dot(left, right, preferred_element_type=jnp.float32)  30.2 us
    ppermute x5, waiting for transfers between devices, traded(): got = lax.ppermute(given, 'pair', [(0, 1), (1, 0)])  16.7 us
    ppermute x1, waiting for transfers between devices, per_device(): mine_before = lax.ppermute(mine, 'hi', onward)  9.64 us
    ppermute x5, starting transfers between devices, traded(): got = lax.ppermute(given, 'pair', [(0, 1), (1, 0)])  8.93 us
    dot_general x2, matrix products, attend(): jnp.einsum('gqc,cd->qgd', weights, values, preferred_element_type=jnp.flo...  7.33 us
  transfers between devices with their start and end apart: 13, of which 7 were waited for; matrix products, arithmetic and copies ran while one was open for 15% of the time, Pallas kernels for 34%

commit v1 on v0

v1 whole, which is shorter than its diff:
```python
import functools

import jax
import jax.numpy as jnp
from jax import lax
from jax.experimental import pallas as pl
from jax.experimental.pallas import tpu as pltpu
from jax.sharding import Mesh, PartitionSpec as P

HEAD_DIM = 128
WINDOW = 1024
LOG2E = 1.4426950408889634
LANES = 128


def product_t(left, right):
    dims = (((1,), (1,)), ((), ()))
    return lax.dot_general(left, right, dims, preferred_element_type=jnp.float32)


def layer_kernel(
    planes, chips, x_ref, gain1, gain2, attn_w, mlp_w, out_ref,
    afull, mfull, mtrade_ref, held1, held2, nbuf, qbuf, kv, att, hidden,
    given, near, stage, far, stream, leave, arrive,
    at_s, at_r, az_s, az_r, mt_s, mt_r, mz_s, mz_r, loc,
    g_s, g_r, gp_s, gp_r, kv_s, kv_r, zx_s, zx_r, rn_s, rn_r, rf_s, rf_r,
):
    rows, cols = x_ref.shape
    depth = attn_w.shape[1]
    heads_w = qbuf.shape[1]
    qkv_w = heads_w + HEAD_DIM
    gu_w = 2 * hidden.shape[1]
    count = 2 * chips
    h, p, t = lax.axis_index("hi"), lax.axis_index("pair"), lax.axis_index("tensor")
    sib = t + 1 - 2 * lax.rem(t, 2)
    other = 1 - p
    parity = lax.rem(h, 2)
    partner = h + 1 - 2 * parity
    finish = []

    def dev(a, b, c):
        return {"hi": a, "pair": b, "tensor": c}

    def sent(source, target, send, recv, where):
        return pltpu.make_async_remote_copy(
            src_ref=source, dst_ref=target, send_sem=send, recv_sem=recv, device_id=where
        )

    def go(copy, cond=None):
        if cond is None:
            copy.start()
            finish.append(copy.wait_send)
        else:
            pl.when(cond)(lambda: copy.start())
            finish.append(lambda: pl.when(cond)(lambda: copy.wait_send()))

    def ahead(k, start):
        return lax.rem(p + k // chips, 2), lax.rem(start + 2 * (k % chips), count)

    def behind(k, start):
        turn = count - 2 * (k % chips)
        return lax.rem(p + k // chips, 2), lax.rem(start + turn, count)

    barrier = pltpu.get_barrier_semaphore()
    for k in range(1, count):
        there = ahead(k, t)
        pl.semaphore_signal(barrier, inc=1, device_id=dev(h, *there))
    pl.semaphore_signal(barrier, inc=1, device_id=dev(h, p, sib))
    for d in range(1, planes):
        pl.semaphore_signal(barrier, inc=1, device_id=dev(lax.rem(h + d, planes), p, t))
    pl.semaphore_signal(barrier, inc=1, device_id=dev(lax.rem(h + 1, planes), other, t))
    pl.semaphore_signal(barrier, inc=1, device_id=dev(lax.rem(h + planes - 1, planes), other, t))
    pl.semaphore_wait(barrier, count + planes + 1)

    parts = (pl.ds(0, qkv_w), pl.ds(qkv_w, attn_w.shape[2] - qkv_w))
    mparts = (pl.ds(0, gu_w), pl.ds(gu_w, mlp_w.shape[3] - gu_w))

    def at_rows(a, b):
        return pl.ds(pl.multiple_of((a * 2 + b) * depth, depth), depth)

    def atrade(part):
        return sent(
            attn_w.at[other, :, parts[part]],
            afull.at[at_rows(h, p), parts[part]],
            at_s.at[part], at_r.at[part], dev(h, other, t),
        )

    def atrade_wait(part):
        place = afull.at[at_rows(h, other), parts[part]]
        sent(place, place, at_s.at[part], at_r.at[part], dev(h, other, t)).wait_recv()

    def a_slice(src, j, part):
        return afull.at[at_rows(src, j), parts[part]]

    def a_send(k, j, part, own=False):
        for way in range(2):
            src = h - k if way == 0 else h + k
            to = h + 1 if way == 0 else h - 1
            cond = (src >= 0) & (to < planes) if way == 0 else (src < planes) & (to >= 0)
            safe = jnp.clip(src, 0, planes - 1)
            source = attn_w.at[p, :, parts[part]] if own else a_slice(safe, j, part)
            go(
                sent(
                    source, a_slice(safe, j, part),
                    az_s.at[way, k, j, part], az_r.at[safe, j, part],
                    dev(jnp.clip(to, 0, planes - 1), p, t),
                ),
                cond,
            )

    def a_wait(k, part):
        for way in range(2):
            src = h - k if way == 0 else h + k
            cond = src >= 0 if way == 0 else src < planes
            safe = jnp.clip(src, 0, planes - 1)
            for j in range(2):
                place = a_slice(safe, j, part)
                copy = sent(
                    place, place, az_s.at[way, k, j, part], az_r.at[safe, j, part], dev(h, p, t)
                )
                pl.when(cond)(lambda copy=copy: copy.wait_recv())

    def a_relay(k, part):
        a_wait(k, part)
        for j in range(2):
            a_send(k, j, part)

    def block(hold, where):
        return hold.at[
            pl.ds(pl.multiple_of(where[0] * rows, rows), rows),
            pl.ds(pl.multiple_of(where[1] * cols, cols), cols),
        ]

    def gather_start(n, source, hold):
        mine = block(hold, (p, t))
        for k in range(count - 1, 0, -1):
            go(sent(source, mine, g_s.at[n, k], g_r.at[n, k], dev(h, *ahead(k, t))))
        go(sent(source, mine, gp_s.at[n, 0], gp_r.at[n, 0], dev(h, p, sib)))
        pltpu.make_async_copy(source, mine, loc.at[n]).start()

    def gather_pass(n, k, hold):
        came = block(hold, behind(k, t))
        sent(came, came, g_s.at[n, k], g_r.at[n, k], dev(h, p, sib)).wait_recv()
        go(sent(came, came, gp_s.at[n, k], gp_r.at[n, k], dev(h, p, sib)))

    def gather_end(n, source, hold):
        pltpu.make_async_copy(source, block(hold, (p, t)), loc.at[n]).wait()
        for k in range(count):
            came = block(hold, behind(k, sib))
            sent(came, came, gp_s.at[n, k], gp_r.at[n, k], dev(h, p, sib)).wait_recv()

    def mtrade(g, part):
        return sent(
            mlp_w.at[other, g, :, mparts[part]],
            mtrade_ref.at[g, :, mparts[part]],
            mt_s.at[g, part], mt_r.at[g, part], dev(h, other, t),
        )

    def m_slice(src, j, part):
        return mfull.at[at_rows(src, j), mparts[part]]

    def m_send(to, cond, traded, part):
        safe = jnp.clip(to, 0, planes - 1)
        g = lax.rem(safe, 2)
        j = other if traded else p
        source = mtrade_ref.at[g, :, mparts[part]] if traded else mlp_w.at[p, g, :, mparts[part]]
        go(
            sent(
                source, m_slice(h, j, part),
                mz_s.at[safe, j, part], mz_r.at[h, j, part], dev(safe, p, t),
            ),
            cond,
        )

    def m_up(traded, part):
        for d in range(planes - 1, 0, -1):
            m_send(h + d, h + d < planes, traded, part)

    def m_down(traded, part):
        for d in range(planes - 1, 0, -1):
            m_send(h - d, h - d >= 0, traded, part)

    def m_wait(part):
        for d in range(1, planes):
            src = lax.rem(h + d, planes)
            for j in range(2):
                place = m_slice(src, j, part)
                sent(
                    place, place, mz_s.at[src, j, part], mz_r.at[src, j, part], dev(h, p, t)
                ).wait_recv()

    for part in range(2):
        go(atrade(part))
    gather_start(0, x_ref, held1)
    for part in range(2):
        a_send(0, p, part, own=True)
    own_a = pltpu.make_async_copy(attn_w.at[p], afull.at[at_rows(h, p), :], loc.at[3])
    own_m = pltpu.make_async_copy(
        mlp_w.at[p, parity], mfull.at[at_rows(h, p), :], loc.at[4]
    )
    for part in range(2):
        atrade_wait(part)
        a_send(0, other, part)
    own_a.start()
    own_m.start()

    @pl.when(h == 0)
    def _():
        kv[:, 0 : 2 * rows, :] = jnp.zeros((2, 2 * rows, HEAD_DIM), kv.dtype)

    a_relay(1, 0)
    gather_pass(0, 1, held1)
    for k in range(2, planes - 1):
        a_relay(k, 0)
    if planes > 2:
        a_relay(1, 1)
    for k in range(2, count):
        gather_pass(0, k, held1)
    go(mtrade(0, 0))
    m_down(False, 0)
    gather_end(0, x_ref, held1)
    a_wait(planes - 1, 0)
    own_a.wait()

    step = 32
    chunk = nbuf.shape[0]

    def norm_chunk(hold, start, gain):
        @pl.loop(0, chunk // step)
        def _(index):
            source = pl.ds(pl.multiple_of(start + index * step, step), step)
            values = hold[source, :].astype(jnp.float32)
            mean_square = jnp.mean(values * values, axis=1, keepdims=True)
            scaled = values * lax.rsqrt(mean_square + 1e-06) * gain[...]
            nbuf[pl.ds(pl.multiple_of(index * step, step), step), :] = scaled.astype(nbuf.dtype)

    scale = HEAD_DIM ** (-0.5) * LOG2E
    chunks = 2 * rows // chunk

    def kv_copies(i):
        mine = kv.at[p, pl.ds(2 * rows + i * chunk, chunk), :]
        before = kv.at[p, pl.ds(i * chunk, chunk), :]
        up = jnp.minimum(h + 1, planes - 1)
        return (
            sent(mine, before, kv_s.at[1, i], kv_r.at[1, i], dev(up, p, t)),
            sent(mine, before, kv_s.at[2, i], kv_r.at[2, i], dev(up, other, t)),
            sent(mine, mine, kv_s.at[0, i], kv_r.at[0, i], dev(h, other, t)),
        )

    for i in range(chunks):
        norm_chunk(held1, i * chunk, gain1)
        made = jnp.dot(nbuf[...], afull[:, 0:qkv_w], preferred_element_type=jnp.float32)
        qbuf[i * chunk : (i + 1) * chunk, :] = (made[:, :heads_w] * scale).astype(qbuf.dtype)
        kv[p, 2 * rows + i * chunk : 2 * rows + (i + 1) * chunk, :] = made[:, heads_w:].astype(
            kv.dtype
        )
        first, second, across = kv_copies(i)
        go(first, h < planes - 1)
        go(second, h < planes - 1)
        go(across)

    for k in range(2, planes - 1):
        a_relay(k, 1)
    m_up(False, 0)
    go(mtrade(1, 0))
    go(mtrade(0, 1))
    go(mtrade(1, 1))

    def kv_waits(i):
        theirs = kv.at[other, pl.ds(2 * rows + i * chunk, chunk), :]
        sent(theirs, theirs, kv_s.at[0, i], kv_r.at[0, i], dev(h, other, t)).wait_recv()

        @pl.when(h > 0)
        def _():
            for way, which in ((1, p), (2, other)):
                before = kv.at[which, pl.ds(i * chunk, chunk), :]
                sent(before, before, kv_s.at[way, i], kv_r.at[way, i], dev(h, p, t)).wait_recv()

    for i in range(chunks):
        kv_waits(i)

    qrows = 256
    edge = WINDOW

    @pl.loop(0, 2 * rows // qrows)
    def _(i):
        base = pl.multiple_of(i * qrows, qrows)
        for head in range(heads_w // HEAD_DIM):
            lanes = slice(head * HEAD_DIM, (head + 1) * HEAD_DIM)
            q = qbuf[pl.ds(base, qrows), lanes]

            def span(which, lo, size):
                return kv[which, pl.ds(pl.multiple_of(base + lo, qrows), size), :]

            s0 = product_t(q, span(0, 0, qrows))
            s1 = product_t(q, span(0, qrows, edge - qrows))
            s2 = product_t(q, span(0, edge, qrows))
            r = lax.broadcasted_iota(jnp.int32, (qrows, qrows), 0)
            c = lax.broadcasted_iota(jnp.int32, (qrows, qrows), 1)
            s0 = jnp.where((c > r) & (h > 0), s0, -1e30)
            s2 = jnp.where(c <= r, s2, -1e30)
            c1 = lax.broadcasted_iota(jnp.int32, (1, edge - qrows), 1) + (base + qrows)
            s1 = s1 + jnp.where((c1 < edge) & (h == 0), -1e30, 0.0)
            top = jnp.maximum(
                jnp.max(s1, axis=1, keepdims=True),
                jnp.maximum(
                    jnp.max(s0, axis=1, keepdims=True), jnp.max(s2, axis=1, keepdims=True)
                ),
            )
            e0, e1, e2 = (jnp.exp2(s - top) for s in (s0, s1, s2))
            total = (
                jnp.sum(e0, axis=1, keepdims=True)
                + jnp.sum(e1, axis=1, keepdims=True)
                + jnp.sum(e2, axis=1, keepdims=True)
            )
            mixed = jnp.dot(
                e0.astype(jnp.bfloat16), span(1, 0, qrows), preferred_element_type=jnp.float32
            )
            mixed += jnp.dot(
                e1.astype(jnp.bfloat16),
                span(1, qrows, edge - qrows),
                preferred_element_type=jnp.float32,
            )
            mixed += jnp.dot(
                e2.astype(jnp.bfloat16), span(1, edge, qrows), preferred_element_type=jnp.float32
            )
            att[pl.ds(base, qrows), lanes] = (mixed / total).astype(att.dtype)

    half = rows // 2
    nt = 64

    def term(left, first, width, right, lo, where, i):
        part = left[pl.ds(pl.multiple_of(first + where[0] * rows + i * half, half), half), :]
        wide = right[pl.ds(pl.multiple_of(where[1] * cols, cols), cols), lo : lo + width]
        return product_t(part, wide)

    def sums(n, left, first, width, right, lo):
        order = list(range(count - 1, -1, -1))
        for k in order:
            for i in range(2):
                value = term(left, first, width, right, lo, ahead(k, sib), i)
                given[n, k, i * half : (i + 1) * half, :] = value.astype(given.dtype)
            go(sent(given.at[n, k], near.at[n, k], rn_s.at[n, k], rn_r.at[n, k], dev(h, p, sib)))
        for k in order:
            came = near.at[n, k]
            sent(came, came, rn_s.at[n, k], rn_r.at[n, k], dev(h, p, sib)).wait_recv()
            for i in range(2):
                value = term(left, first, width, right, lo, ahead(k, t), i)
                at = slice(i * half, (i + 1) * half)
                value = value + near[n, k, at, :].astype(jnp.float32)
                stage[n, k, at, :] = value.astype(stage.dtype)
            if k:
                go(
                    sent(
                        stage.at[n, k], far.at[n, k], rf_s.at[n, k], rf_r.at[n, k],
                        dev(h, *ahead(k, t)),
                    )
                )

    def sums_end(n, extra, target):
        for k in range(1, count):
            came = far.at[n, k]
            sent(came, came, rf_s.at[n, k], rf_r.at[n, k], dev(h, p, t)).wait_recv()

        @pl.loop(0, rows // nt)
        def _(index):
            part = pl.ds(pl.multiple_of(index * nt, nt), nt)
            total = stage[n, 0, part, :].astype(jnp.float32)
            for k in range(1, count):
                total = total + far[n, k, part, :].astype(jnp.float32)
            for ref in extra:
                total = total + ref[part, :].astype(jnp.float32)
            target[part, :] = total.astype(target.dtype)

    for k in range(1, planes):
        if k == planes - 1 or planes <= 2:
            a_wait(k, 1)
    sums(0, att, 0, heads_w, afull, qkv_w)
    sums_end(0, (x_ref,), stream)

    give = sent(stream, arrive.at[0], zx_s.at[0], zx_r.at[0], dev(partner, p, t))
    go(give)
    gather_start(1, stream, held2.at[0])
    own_m.wait()
    for g in range(2):
        place = mtrade_ref.at[g, :, mparts[0]]
        sent(place, place, mt_s.at[g, 0], mt_r.at[g, 0], dev(h, other, t)).wait_recv()
    m_up(True, 0)
    m_down(True, 0)
    for g in range(2):
        place = mtrade_ref.at[g, :, mparts[1]]
        sent(place, place, mt_s.at[g, 1], mt_r.at[g, 1], dev(h, other, t)).wait_recv()
    kept = pltpu.make_async_copy(
        mtrade_ref.at[parity], mfull.at[at_rows(h, other), :], loc.at[3]
    )
    kept.start()
    for traded in (False, True):
        m_up(traded, 1)
        m_down(traded, 1)
    give.wait_recv()
    gather_start(2, arrive.at[0], held2.at[1])
    for k in range(1, count):
        gather_pass(1, k, held2.at[0])
    gather_end(1, stream, held2.at[0])
    kept.wait()
    m_wait(0)

    units = hidden.shape[1]

    def mlp_chunk(plane, i):
        norm_chunk(held2.at[plane], i * chunk, gain2)
        made = jnp.dot(nbuf[...], mfull[:, 0:gu_w], preferred_element_type=jnp.float32)
        gate, up = made[:, :units], made[:, units:]
        value = gate / (1.0 + jnp.exp(-gate)) * up
        hidden[plane * 2 * rows + i * chunk : plane * 2 * rows + (i + 1) * chunk, :] = value.astype(
            hidden.dtype
        )

    for i in range(chunks):
        mlp_chunk(0, i)
    for k in range(1, count):
        gather_pass(2, k, held2.at[1])
    gather_end(2, arrive.at[0], held2.at[1])
    for i in range(chunks):
        mlp_chunk(1, i)
    m_wait(1)

    sums(1, hidden, 2 * rows, units, mfull, gu_w)
    sums(2, hidden, 0, units, mfull, gu_w)
    sums_end(1, (), leave)
    back = sent(leave, arrive.at[1], zx_s.at[1], zx_r.at[1], dev(partner, p, t))
    go(back)
    for wait in finish[:-1]:
        wait()
    back.wait_recv()
    sums_end(2, (stream, arrive.at[1]), out_ref)
    finish[-1]()


def per_device(tokens, attn_gain, w_query, w_key, w_value, w_out, mlp_gain, w_gate, w_up, w_down):
    rows, cols = tokens.shape
    planes = lax.axis_size("hi")
    chips = lax.axis_size("tensor") // 2
    count = 2 * chips
    depth = w_query.shape[0]
    width = cols * count
    heads_w = w_query.shape[1] // 2
    units = w_gate.shape[1] // 4
    padded = -(-units // LANES) * LANES

    attn_w = []
    for j, extra in enumerate((w_key, w_value)):
        cut = slice(j * heads_w, (j + 1) * heads_w)
        attn_w.append(jnp.concatenate([w_query[:, cut], extra, w_out[cut].T], axis=1))
    attn_w = jnp.stack(attn_w)
    fill = ((0, 0), (0, padded - units))
    mlp_w = []
    for j in range(4):
        cut = slice(j * units, (j + 1) * units)
        pieces = [w_gate[:, cut], w_up[:, cut], w_down[cut].T]
        mlp_w.append(jnp.concatenate([jnp.pad(piece, fill) for piece in pieces], axis=1))
    mlp_w = jnp.stack(mlp_w).reshape(2, 2, depth, 3 * padded)

    bf16 = jnp.bfloat16
    vmem = pl.BlockSpec(memory_space=pltpu.VMEM)
    blocks = pltpu.VMEM((3, count, rows, cols), bf16)
    share = pltpu.VMEM((rows, cols), bf16)
    chunk = rows // 2
    chunks = 2 * rows // chunk
    dma = pltpu.SemaphoreType.DMA
    return pl.pallas_call(
        functools.partial(layer_kernel, planes, chips),
        out_shape=jax.ShapeDtypeStruct((rows, cols), bf16),
        in_specs=[vmem] * 5,
        out_specs=vmem,
        scratch_shapes=[
            pltpu.VMEM((width, attn_w.shape[2]), bf16),
            pltpu.VMEM((width, mlp_w.shape[3]), bf16),
            pltpu.VMEM((2, depth, mlp_w.shape[3]), bf16),
            pltpu.VMEM((2 * rows, width), bf16),
            pltpu.VMEM((2, 2 * rows, width), bf16),
            pltpu.VMEM((chunk, width), bf16),
            pltpu.VMEM((2 * rows, heads_w), bf16),
            pltpu.VMEM((2, 4 * rows, HEAD_DIM), bf16),
            pltpu.VMEM((2 * rows, heads_w), bf16),
            pltpu.VMEM((4 * rows, padded), bf16),
            blocks, blocks, blocks, blocks,
            share, share,
            pltpu.VMEM((2, rows, cols), bf16),
            dma((2,)), dma((2,)),
            dma((2, planes, 2, 2)), dma((planes, 2, 2)),
            dma((2, 2)), dma((2, 2)),
            dma((planes, 2, 2)), dma((planes, 2, 2)),
            dma((5,)),
            dma((3, count)), dma((3, count)), dma((3, count)), dma((3, count)),
            dma((3, chunks)), dma((3, chunks)),
            dma((2,)), dma((2,)),
            dma((3, count)), dma((3, count)), dma((3, count)), dma((3, count)),
        ],
        compiler_params=pltpu.CompilerParams(
            collective_id=1, has_side_effects=True, vmem_limit_bytes=66_000_000
        ),
    )(tokens, attn_gain.reshape(1, -1), mlp_gain.reshape(1, -1), attn_w, mlp_w)


def solution(mesh):
    sizes = mesh.shape
    split = Mesh(
        mesh.devices.reshape(sizes["seq"] // 2, 2, sizes["tensor"]), ("hi", "pair", "tensor")
    )
    seq = ("hi", "pair")
    in_specs = (
        P(seq, "tensor"),
        P(),
        P(seq, "tensor"),
        P(seq, "tensor"),
        P(seq, "tensor"),
        P("tensor", seq),
        P(),
        P(seq, "tensor"),
        P(seq, "tensor"),
        P("tensor", seq),
    )
    return jax.shard_map(
        per_device, mesh=split, in_specs=in_specs, out_specs=P(seq, "tensor"), check_vma=False
    )
```

time: 312 us -> 241 us (0.77)
  Pallas kernels: 138 us -> 222 us
  waiting for transfers between devices: 80.6 us -> 0 us
  matrix products: 43.5 us -> 0 us
  starting transfers between devices: 18.1 us -> 0 us
  between operations: 13.4 us -> 0.17 us
  other arithmetic: 10.2 us -> 3.54 us
  local copies, waits for them, and re-layouts: 7.57 us -> 13.3 us
    pallas_call x4 -> x1, Pallas kernels: 138 us -> 222 us  [per_device(): pl.pallas_call(functools.partial(layer_kernel, planes, chips), out_shape=...]
    all_gather x4 -> x0, waiting for transfers between devices: 47.5 us -> none  [the longest x1 47.5 us: per_device(): down_full = lax.all_gather(traded(w_down, 0), 'hi', axis=1, tiled=True)]
    dot_general x6 -> x0, matrix products: 37.5 us -> none  [the longest x4 30.2 us: product(): return jnp.dot(left, right, preferred_element_type=jnp.float32)]
    ppermute x9 -> x0, waiting for transfers between devices: 33 us -> none  [the longest x5 16.7 us: traded(): got = lax.ppermute(given, 'pair', [(0, 1), (1, 0)])]
    ppermute x9 -> x0, starting transfers between devices: 18 us -> none  [the longest x5 8.93 us: traded(): got = lax.ppermute(given, 'pair', [(0, 1), (1, 0)])]
    sub x2 -> x0, matrix products: 6 us -> none  [attend(): raised = jnp.exp(scores - highest)]
    unnamed x10 -> x31, local copies, waits for them, and re-layouts: 2.85 us -> 8.02 us
    select_n x7 -> x0, other arithmetic: 4.64 us -> none  [the longest x4 2.71 us: traded(): jnp.where(first, kept, got)]
  transfers between devices with their start and end apart: 13 -> 0, of which waited for: 7 -> 0; matrix products, arithmetic and copies ran while one was open for 15% -> 0% of each run, Pallas kernels for 34% -> 0%
where the time goes in v1:
time: 241 us; the launch traced here: 239 us
  Pallas kernels  222 us (92%)
  local copies, waits for them, and re-layouts  13.3 us (6%)
  other arithmetic  3.54 us (1%)
    pallas_call x1, Pallas kernels, per_device(): pl.pallas_call(functools.partial(layer_kernel, planes, chips), out_shape=...  222 us
    unnamed x31, local copies, waits for them, and re-layouts  8.02 us

profile of v1, /device:TPU:0, one launch (start us, length us, event | category | flops | bytes accessed | tf_op | source)
XLA Modules:
  0.0 238.8 jit_solution(15714098511947493708)
XLA Ops:
  0.0 2.2 slice_bitcast_fusion.3
  2.2 0.3 fusion.22
  2.4 0.8 copy.26
  3.2 0.3 fusion.23
  3.5 0.8 copy.27
  4.3 0.8 copy.28
  5.1 0.8 copy.29
  6.0 1.4 fusion.13
  7.4 0.8 copy.30
  8.2 0.8 copy.31
  9.0 0.1 copy.24
  9.2 0.1 copy.25
  9.3 0.8 broadcast_select_fusion.1
  10.2 0.0 copy-done.5
  10.2 0.1 fusion.19
  10.3 0.3 pad_maximum_fusion
  10.6 2.5 %copy.21 = bf16[4,256,1152]{2,1,0:T(8,128)(2,1)} copy(bf16[4,256,1152]{1,2,0:T(8,128)(2,1)S(1)} %pad_maximum_fusion) | data formatting | bytes 4718592 | tf_op jit(solution)/shard_map/stack | solution.py:462
  13.1 0.1 copy.22
  13.2 0.1 copy.23
  13.4 0.7 copy-done.7
  14.1 0.1 maximum_bitcast_fusion
  14.2 0.9 pad_maximum_fusion.1.attn_w
  15.1 221.8 %shard_map.100 = bf16[512,512]{1,0:T(8,128)(2,1)} custom-call(bf16[512,512]{1,0:T(8,128)(2,1)} %x_ref.1, f32[1,2048]{1,0:T(1,128)} %bitcast.28, f32[1,2048]{1,0:T(1,128)} %bitcast.29, bf16[2,256,640]{2,1,0:T(8,128)(2,1)} %pad_maximum_fusion.1.attn_w, bf16[2,2,256,1152]{3,2,1,0:T(8,128)(2,1)} %bitcast.25), custom_call_target="tpu_custom_call" | custom-call | tf_op jit(solution)/shard_map/pallas_call | solution.py:471
  236.9 1.9 copy.33
  (24 shorter events, 0.1 us)
Async XLA Ops:
  0.0 2.2 copy-start
  0.0 3.2 %copy-start.1 = (bf16[256,1408]{1,0:T(8,128)(2,1)S(1)}, bf16[256,1408]{1,0:T(8,128)(2,1)}, u32[]{:S(2)}) copy-start(bf16[256,1408]{1,0:T(8,128)(2,1)} %param.18) | copy-start | bytes 2162692
  6.0 3.1 %slice-start = ((bf16[256,1408]{1,0:T(8,128)(2,1)}), bf16[256,384]{1,0:T(8,128)(2,1)S(1)}, s32[]{:S(2)}) async-start(bf16[256,1408]{1,0:T(8,128)(2,1)} %param.17), calls=%async_computation | async-start | bytes 393216 | tf_op jit(solution)/shard_map/slice
  7.4 1.8 slice-start.1
  9.0 1.1 copy-start.2
  9.0 1.1 copy-start.3
  9.0 1.1 copy-start.4
  9.0 1.2 copy-start.5
  10.6 2.5 %copy-start.6 = (bf16[512,256]{1,0:T(8,128)(2,1)S(1)}, bf16[512,256]{1,0:T(8,128)(2,1)}, u32[]{:S(2)}) copy-start(bf16[512,256]{1,0:T(8,128)(2,1)} %param.15) | copy-start | bytes 786436
  13.1 0.9 copy-start.7
  13.1 1.0 copy-start.8
  13.1 1.0 copy-start.9

commit v2 on v1

v2 whole, which is shorter than its diff:
```python
import functools

import jax
import jax.numpy as jnp
from jax import lax
from jax.experimental import pallas as pl
from jax.experimental.pallas import tpu as pltpu
from jax.sharding import Mesh, PartitionSpec as P

HEAD_DIM = 128
WINDOW = 1024
LOG2E = 1.4426950408889634
LANES = 128


def product_t(left, right):
    dims = (((1,), (1,)), ((), ()))
    return lax.dot_general(left, right, dims, preferred_element_type=jnp.float32)


def layer_kernel(
    planes, chips, x_ref, gain1, gain2, wq, wk, wv, wo, wg, wu, wd, out_ref,
    qkv_full, wo_full, gu_own, gu_full, gu_trade, wd_full, wd_trade, held1, held2, nbuf, qbuf, kv, att, hidden,
    given, near, stage, far, stream, leave, arrive,
    at_s, at_r, az_s, az_r, mt_s, mt_r, mz_s, mz_r, loc, kept,
    g_s, g_r, gp_s, gp_r, kv_s, kv_r, zx_s, zx_r, rn_s, rn_r, rf_s, rf_r,
):
    rows, cols = x_ref.shape
    half = rows // 2
    depth = wq.shape[0]
    heads_w = qbuf.shape[1]
    units, padded = wd.shape[0] // 4, hidden.shape[1]
    gu_w = 2 * padded
    count = 2 * chips
    h, p, t = lax.axis_index("hi"), lax.axis_index("pair"), lax.axis_index("tensor")
    core = lax.rem(t, 2)
    sib = t + 1 - 2 * core
    near_k, far_k = 1 + core, 2 - core
    halves = (pl.ds(0, x_ref.shape[0] // 2), pl.ds(x_ref.shape[0] // 2, x_ref.shape[0] // 2))
    other = 1 - p
    parity = lax.rem(h, 2)
    partner = h + 1 - 2 * parity
    finish = []
    scopes = []

    def mark(name):
        if scopes:
            scopes.pop().__exit__(None, None, None)
        if name:
            scopes.append(jax.named_scope(name))
            scopes[-1].__enter__()

    def dev(a, b, c):
        return {"hi": a, "pair": b, "tensor": c}

    def sent(source, target, send, recv, where):
        return pltpu.make_async_remote_copy(
            src_ref=source, dst_ref=target, send_sem=send, recv_sem=recv, device_id=where
        )

    def go(copy, cond=None):
        if cond is None:
            copy.start()
            finish.append(copy.wait_send)
        else:
            pl.when(cond)(lambda: copy.start())
            finish.append(lambda: pl.when(cond)(lambda: copy.wait_send()))

    def ahead(k, start):
        shift, turn = lax.div(k, 2), lax.rem(k, 2)
        return lax.rem(p + shift, 2), lax.rem(start + 2 * turn, count)

    mark("barrier")
    barrier = pltpu.get_barrier_semaphore()
    for k in range(1, count):
        there = ahead(k, t)
        pl.semaphore_signal(barrier, inc=1, device_id=dev(h, *there))
    pl.semaphore_signal(barrier, inc=1, device_id=dev(h, p, sib))
    for d in range(1, planes):
        pl.semaphore_signal(barrier, inc=1, device_id=dev(lax.rem(h + d, planes), p, t))
    pl.semaphore_signal(barrier, inc=1, device_id=dev(lax.rem(h + 1, planes), other, t))
    pl.semaphore_signal(barrier, inc=1, device_id=dev(lax.rem(h + planes - 1, planes), other, t))
    pl.semaphore_wait(barrier, count + planes + 1)

    def at_rows(a, b):
        return pl.ds(pl.multiple_of((a * 2 + b) * depth, depth), depth)

    def q_cols(which):
        return pl.ds(pl.multiple_of(which * heads_w, heads_w), heads_w)

    def d_rows(which, g):
        return pl.ds(pl.multiple_of((which * 2 + g) * units, 32), units)

    q_place, kv_place = pl.ds(0, heads_w), pl.ds(heads_w, HEAD_DIM)
    across = dev(h, other, t)

    def qkv_trade():
        place = qkv_full.at[at_rows(h, p), :]
        q_copy = sent(wq.at[:, q_cols(other)], place.at[:, q_place], at_s.at[0], at_r.at[0], across)
        k_copy, v_copy = (
            sent(ref, place.at[:, kv_place], at_s.at[1], at_r.at[1], across) for ref in (wk, wv)
        )
        go(q_copy)
        go(k_copy, p == 1)
        go(v_copy, p == 0)

    def qkv_trade_wait():
        place = qkv_full.at[at_rows(h, other), :]
        for n, lanes in ((0, q_place), (1, kv_place)):
            came = place.at[:, lanes]
            sent(came, came, at_s.at[n], at_r.at[n], across).wait_recv()

    def qkv_own():
        place = qkv_full.at[at_rows(h, p), :]
        q_copy = pltpu.make_async_copy(wq.at[:, q_cols(p)], place.at[:, q_place], loc.at[3, 0])
        k_copy, v_copy = (
            pltpu.make_async_copy(ref, place.at[:, kv_place], loc.at[3, 1]) for ref in (wk, wv)
        )
        q_copy.start()
        pl.when(p == 0)(lambda: k_copy.start())
        pl.when(p == 1)(lambda: v_copy.start())
        q_copy.wait()
        k_copy.wait()

    def wo_trade():
        return sent(
            wo.at[q_cols(other), :], wo_full.at[h * 2 + p], at_s.at[2], at_r.at[2], across
        )

    def wo_trade_wait():
        came = wo_full.at[h * 2 + other]
        sent(came, came, at_s.at[2], at_r.at[2], across).wait_recv()

    def a_slice(src, j, part):
        if part:
            return wo_full.at[src * 2 + j]
        return qkv_full.at[at_rows(src, j), :]

    def a_hop(k, way):
        src, to = (h - k, h + 1) if way == 0 else (h + k, h - 1)
        held = src >= 0 if way == 0 else src < planes
        onward = to < planes if way == 0 else to >= 0
        return jnp.clip(src, 0, planes - 1), jnp.clip(to, 0, planes - 1), held, onward

    def a_send(k, j, part, own=False, ways=(0, 1)):
        for way in ways:
            src, to, held, onward = a_hop(k, way)
            source = wo.at[q_cols(p), :] if own and part else a_slice(src, j, part)
            go(
                sent(
                    source, a_slice(src, j, part),
                    az_s.at[way, k, j, part], az_r.at[src, j, part], dev(to, p, t),
                ),
                held & onward,
            )

    def a_wait(k, part, way, last):
        src, to, held, onward = a_hop(k, way)
        cond = held & jnp.logical_not(onward) if last else held & onward
        for j in range(2):
            place = a_slice(src, j, part)
            copy = sent(place, place, az_s.at[way, k, j, part], az_r.at[src, j, part], dev(h, p, t))
            pl.when(cond)(lambda copy=copy: copy.wait_recv())

    def a_relay(k, part):
        for way in range(2):
            a_wait(k, part, way, False)
            for j in range(2):
                a_send(k, j, part, ways=(way,))

    def a_finish(part):
        for k in range(1, planes):
            for way in range(2):
                a_wait(k, part, way, True)

    def block(hold, where, i):
        return hold.at[
            pl.ds(pl.multiple_of(where[0] * rows + i * half, half), half),
            pl.ds(pl.multiple_of(where[1] * cols, cols), cols),
        ]

    def gather_start(n, i, source, hold):
        mine = block(hold, (p, t), i)
        source = source.at[halves[i]]
        for k in (near_k, far_k):
            go(sent(source, mine, g_s.at[n, k, i], g_r.at[n, k, i], dev(h, *ahead(k, t))))
        go(sent(source, mine, gp_s.at[n, 0, i], gp_r.at[n, 0, i], dev(h, p, sib)))
        pltpu.make_async_copy(source, mine, loc.at[n, i]).start()

    def gather_pass(n, i, k, hold, relay=False):
        came = block(hold, ahead(k, t), i)
        sent(came, came, g_s.at[n, k, i], g_r.at[n, k, i], dev(h, p, sib)).wait_recv()
        if relay:
            go(sent(came, came, g_s.at[n, 3, i], g_r.at[n, 3, i], dev(h, *ahead(near_k, t))))
        go(sent(came, came, gp_s.at[n, k, i], gp_r.at[n, k, i], dev(h, p, sib)))

    def gather_relay(n, hold):
        for i in range(2):
            gather_pass(n, i, far_k, hold, relay=True)

    def gather_rest(n, i, source, hold):
        gather_pass(n, i, near_k, hold)
        gather_pass(n, i, 3, hold)
        mine = block(hold, (p, t), i)
        pltpu.make_async_copy(source.at[halves[i]], mine, loc.at[n, i]).wait()
        for k in range(count):
            came = block(hold, ahead(k, sib), i)
            sent(came, came, gp_s.at[n, k, i], gp_r.at[n, k, i], dev(h, p, sib)).wait_recv()

    def mtrade(g, part):
        source = wd.at[d_rows(other, g), :] if part else gu_own.at[other, g]
        target = wd_trade.at[g] if part else gu_trade.at[g]
        return sent(source, target, mt_s.at[g, part], mt_r.at[g, part], across)

    def mtrade_wait(g, part):
        came = wd_trade.at[g] if part else gu_trade.at[g]
        sent(came, came, mt_s.at[g, part], mt_r.at[g, part], across).wait_recv()

    def m_slice(src, j, part):
        if part:
            return wd_full.at[src * 2 + j, pl.ds(0, units), :]
        return gu_full.at[at_rows(src, j), :]

    def m_source(traded, g, part):
        if traded:
            return wd_trade.at[g] if part else gu_trade.at[g]
        return wd.at[d_rows(p, g), :] if part else gu_own.at[p, g]

    def m_send(to, cond, traded, part):
        safe = jnp.clip(to, 0, planes - 1)
        j = other if traded else p
        go(
            sent(
                m_source(traded, lax.rem(safe, 2), part), m_slice(h, j, part),
                mz_s.at[safe, j, part], mz_r.at[h, j, part], dev(safe, p, t),
            ),
            cond,
        )

    def m_keep(traded, part):
        j = other if traded else p
        return pltpu.make_async_copy(
            m_source(traded, parity, part), m_slice(h, j, part), kept.at[int(traded), part]
        )

    def m_up(traded, part, also=True):
        for d in range(planes - 1, 0, -1):
            m_send(h + d, (h + d < planes) & also, traded, part)

    def m_down(traded, part, also=True):
        for d in range(planes - 1, 0, -1):
            m_send(h - d, (h - d >= 0) & also, traded, part)

    def m_outward(traded, part):
        m_up(traded, part, parity == 1)
        m_down(traded, part, parity == 0)

    def m_inward(traded, part):
        m_up(traded, part, parity == 0)
        m_down(traded, part, parity == 1)

    def m_wait(part):
        for traded in (False, True):
            m_keep(traded, part).wait()
        for d in range(1, planes):
            src = lax.rem(h + d, planes)
            for j in range(2):
                place = m_slice(src, j, part)
                sent(
                    place, place, mz_s.at[src, j, part], mz_r.at[src, j, part], dev(h, p, t)
                ).wait_recv()

    def pack():
        zeros = jnp.zeros((depth, padded - units), gu_own.dtype)
        for b in range(4):
            lanes = slice(b * units, (b + 1) * units)
            for n, ref in enumerate((wg, wu)):
                gu_own[b // 2, b % 2, :, n * padded : (n + 1) * padded] = jnp.concatenate(
                    [ref[:, lanes], zeros], axis=1
                )

    mark("start")
    qkv_trade()
    qkv_own()
    a_send(0, p, 0)
    for i in range(2):
        gather_start(0, i, x_ref, held1)
    go(wo_trade())
    mark("pack")
    pack()
    mark("trade")
    qkv_trade_wait()
    a_send(0, other, 0)
    own_wo = pltpu.make_async_copy(wo.at[q_cols(p), :], wo_full.at[h * 2 + p], loc.at[4, 0])
    own_wo.start()
    for part in range(2):
        m_keep(False, part).start()
    for s in range(wd_full.shape[0]):
        wd_full[s, units:, :] = jnp.zeros((padded - units, depth), wd_full.dtype)

    @pl.when(h == 0)
    def _():
        kv[:, 0 : 2 * rows, :] = jnp.zeros((2, 2 * rows, HEAD_DIM), kv.dtype)

    mark("relays")
    a_relay(1, 0)
    gather_relay(0, held1)
    for k in range(2, planes - 1):
        a_relay(k, 0)
    a_send(0, p, 1, own=True)
    wo_trade_wait()
    a_send(0, other, 1)
    mark("gather1")
    go(mtrade(0, 0))
    for i in range(2):
        gather_rest(0, i, x_ref, held1)
    mark("a_wait")
    a_finish(0)

    step = 32
    chunk = nbuf.shape[0]

    def norm_chunk(hold, start, size, gain):
        @pl.loop(0, size // step)
        def _(index):
            source = pl.ds(pl.multiple_of(start + index * step, step), step)
            values = hold[source, :].astype(jnp.float32)
            mean_square = jnp.mean(values * values, axis=1, keepdims=True)
            scaled = values * lax.rsqrt(mean_square + 1e-06) * gain[...]
            nbuf[pl.ds(pl.multiple_of(index * step, step), step), :] = scaled.astype(nbuf.dtype)

    scale = HEAD_DIM ** (-0.5) * LOG2E
    chunks = 2 * rows // chunk

    def kv_rows(first, i):
        return pl.ds(first * 2 * rows + i * chunk, chunk)

    def kv_up(i):
        up = jnp.minimum(h + 1, planes - 1)
        mine, before = kv.at[p, kv_rows(1, i), :], kv.at[p, kv_rows(0, i), :]
        return sent(mine, before, kv_s.at[1, i], kv_r.at[1, i], dev(up, p, t))

    def kv_across(which, first, i):
        mine = kv.at[which, kv_rows(first, i), :]
        slot = 2 * (1 - first)
        return sent(mine, mine, kv_s.at[slot, i], kv_r.at[slot, i], across)

    mark("qkv")
    for i in range(chunks):
        if i == 1:
            a_relay(1, 1)
        norm_chunk(held1, i * chunk, chunk, gain1)
        made = jnp.dot(nbuf[...], qkv_full[...], preferred_element_type=jnp.float32)
        qbuf[i * chunk : (i + 1) * chunk, :] = (made[:, :heads_w] * scale).astype(qbuf.dtype)
        kv[p, 2 * rows + i * chunk : 2 * rows + (i + 1) * chunk, :] = made[:, heads_w:].astype(
            kv.dtype
        )
        go(kv_up(i), h < planes - 1)
        go(kv_across(p, 1, i))

    mark("wo_relay")
    for k in range(2, planes - 1):
        a_relay(k, 1)
    m_down(False, 0)
    m_up(False, 0)

    mark("kv_wait")
    for i in range(chunks):
        pl.when(h > 0)(lambda i=i: kv_up(i).wait_recv())
        go(kv_across(p, 0, i), h > 0)
    for i in range(chunks):
        kv_across(other, 1, i).wait_recv()
        pl.when(h > 0)(lambda i=i: kv_across(other, 0, i).wait_recv())
    go(mtrade(1, 0))
    mark("attention")
    qrows = 256
    edge = WINDOW

    @pl.loop(0, 2 * rows // qrows)
    def _(i):
        base = pl.multiple_of(i * qrows, qrows)
        for head in range(heads_w // HEAD_DIM):
            lanes = slice(head * HEAD_DIM, (head + 1) * HEAD_DIM)
            q = qbuf[pl.ds(base, qrows), lanes]

            def span(which, lo, size):
                return kv[which, pl.ds(pl.multiple_of(base + lo, qrows), size), :]

            s0 = product_t(q, span(0, 0, qrows))
            s1 = product_t(q, span(0, qrows, edge - qrows))
            s2 = product_t(q, span(0, edge, qrows))
            r = lax.broadcasted_iota(jnp.int32, (qrows, qrows), 0)
            c = lax.broadcasted_iota(jnp.int32, (qrows, qrows), 1)
            s0 = jnp.where((c > r) & (h > 0), s0, -1e30)
            s2 = jnp.where(c <= r, s2, -1e30)
            c1 = lax.broadcasted_iota(jnp.int32, (1, edge - qrows), 1) + (base + qrows)
            s1 = s1 + jnp.where((c1 < edge) & (h == 0), -1e30, 0.0)
            top = jnp.maximum(
                jnp.max(s1, axis=1, keepdims=True),
                jnp.maximum(
                    jnp.max(s0, axis=1, keepdims=True), jnp.max(s2, axis=1, keepdims=True)
                ),
            )
            e0, e1, e2 = (jnp.exp2(s - top) for s in (s0, s1, s2))
            total = (
                jnp.sum(e0, axis=1, keepdims=True)
                + jnp.sum(e1, axis=1, keepdims=True)
                + jnp.sum(e2, axis=1, keepdims=True)
            )
            mixed = jnp.dot(
                e0.astype(jnp.bfloat16), span(1, 0, qrows), preferred_element_type=jnp.float32
            )
            mixed += jnp.dot(
                e1.astype(jnp.bfloat16),
                span(1, qrows, edge - qrows),
                preferred_element_type=jnp.float32,
            )
            mixed += jnp.dot(
                e2.astype(jnp.bfloat16), span(1, edge, qrows), preferred_element_type=jnp.float32
            )
            att[pl.ds(base, qrows), lanes] = (mixed / total).astype(att.dtype)

    nt = 64

    def term(left, first, width, right, where, i):
        part = left[pl.ds(pl.multiple_of(first + where[0] * rows + i * half, half), half), :]
        made = [
            jnp.dot(
                part, right[where[1] * (cols // depth) + b], preferred_element_type=jnp.float32
            )
            for b in range(cols // depth)
        ]
        return jnp.concatenate(made, axis=1)

    def give(n, k, left, first, width, right):
        for i in range(2):
            value = term(left, first, width, right, ahead(k, sib), i)
            given[n, k, halves[i], :] = value.astype(given.dtype)
            go(
                sent(
                    given.at[n, k, halves[i]], near.at[n, k, halves[i]],
                    rn_s.at[n, k, i], rn_r.at[n, k, i], dev(h, p, sib),
                )
            )

    def own(n, k, i, extra, left, first, width, right):
        came = near.at[n, k, halves[i]]
        sent(came, came, rn_s.at[n, k, i], rn_r.at[n, k, i], dev(h, p, sib)).wait_recv()
        value = term(left, first, width, right, ahead(k, t), i)
        value = value + near[n, k, halves[i], :].astype(jnp.float32)
        if extra:
            landed(n, 3, i).wait_recv()
            value = value + far[n, 3, halves[i], :].astype(jnp.float32)
        stage[n, k, halves[i], :] = value.astype(stage.dtype)

    def onward(n, k, slot, way, i):
        go(
            sent(
                stage.at[n, k, halves[i]], far.at[n, slot, halves[i]],
                rf_s.at[n, slot, i], rf_r.at[n, slot, i], dev(h, *ahead(way, t)),
            )
        )

    def sums_far(n, *terms):
        give(n, 3, *terms)
        give(n, far_k, *terms)
        for i in range(2):
            own(n, 3, i, False, *terms)
            onward(n, 3, 3, near_k, i)

    def sums_near(n, *terms):
        give(n, near_k, *terms)
        for i in range(2):
            own(n, near_k, i, False, *terms)
            onward(n, near_k, near_k, near_k, i)

    def sums_last(n, *terms):
        give(n, 0, *terms)
        for i in range(2):
            own(n, far_k, i, True, *terms)
            onward(n, far_k, far_k, far_k, i)
        for i in range(2):
            own(n, 0, i, False, *terms)

    def landed(n, k, i):
        came = far.at[n, k, halves[i]]
        return sent(came, came, rf_s.at[n, k, i], rf_r.at[n, k, i], dev(h, p, t))

    def sums_end(n, i, extra, target):
        for k in (1, 2):
            landed(n, k, i).wait_recv()

        @pl.loop(0, half // nt)
        def _(index):
            part = pl.ds(pl.multiple_of(i * half + index * nt, nt), nt)
            total = stage[n, 0, part, :].astype(jnp.float32)
            for k in (1, 2):
                total = total + far[n, k, part, :].astype(jnp.float32)
            for ref in extra:
                total = total + ref[part, :].astype(jnp.float32)
            target[part, :] = total.astype(target.dtype)

    mark("trade_wait")
    for g in range(2):
        mtrade_wait(g, 0)
    m_keep(True, 0).start()
    m_outward(True, 0)
    m_outward(False, 1)
    mark("wo_wait")
    a_finish(1)
    mark("sums0")
    own_wo.wait()
    sums_far(0, att, 0, heads_w, wo_full)
    sums_near(0, att, 0, heads_w, wo_full)
    sums_last(0, att, 0, heads_w, wo_full)
    go(mtrade(0, 1))
    go(mtrade(1, 1))
    mark("end0")
    gives = []
    for i in range(2):
        sums_end(0, i, (x_ref,), stream)
        gives.append(
            sent(
                stream.at[halves[i]], arrive.at[0, halves[i]],
                zx_s.at[0, i], zx_r.at[0, i], dev(partner, p, t),
            )
        )
        go(gives[i])
        gather_start(1, i, stream, held2.at[0])
    mark("send2")
    m_inward(True, 0)
    m_inward(False, 1)
    for g in range(2):
        mtrade_wait(g, 1)
    m_keep(True, 1).start()
    m_outward(True, 1)
    m_inward(True, 1)
    mark("zwait")
    gather_relay(1, held2.at[0])
    mark("gather2a")
    for i in range(2):
        gives[i].wait_recv()
        gather_start(2, i, arrive.at[0], held2.at[1])
    for i in range(2):
        gather_rest(1, i, stream, held2.at[0])
    mark("relay2b")
    gather_relay(2, held2.at[1])
    mark("gu_wait")
    m_wait(0)


    def mlp_half(plane, i):
        for run in range(2):
            start = run * rows + i * half
            norm_chunk(held2.at[plane], start, half, gain2)
            made = jnp.dot(nbuf[0:half, :], gu_full[...], preferred_element_type=jnp.float32)
            gate, up = made[:, :padded], made[:, padded:]
            value = gate / (1.0 + jnp.exp(-gate)) * up
            start = plane * 2 * rows + start
            hidden[start : start + half, :] = value.astype(hidden.dtype)

    mark("mlp0")
    for i in range(2):
        mlp_half(0, i)
    for i in range(2):
        mark("gather2b")
        gather_rest(2, i, arrive.at[0], held2.at[1])
        mark("mlp1")
        mlp_half(1, i)
    mark("wd_wait")
    m_wait(1)

    mark("sums1")
    theirs = (1, hidden, 2 * rows, padded, wd_full)
    ours = (2, hidden, 0, padded, wd_full)
    sums_far(*theirs)
    sums_near(*theirs)
    sums_far(*ours)
    mark("sums2")
    sums_last(*theirs)
    sums_near(*ours)
    mark("sums3")
    sums_last(*ours)
    mark("end1")
    backs = []
    for i in range(2):
        sums_end(1, i, (), leave)
        backs.append(
            sent(
                leave.at[halves[i]], arrive.at[1, halves[i]],
                zx_s.at[1, i], zx_r.at[1, i], dev(partner, p, t),
            )
        )
        go(backs[i])
    mark("end2")
    for i in range(2):
        backs[i].wait_recv()
        sums_end(2, i, (stream, arrive.at[1]), out_ref)
    mark("drain")
    for wait in finish:
        wait()
    mark(None)


def per_device(tokens, attn_gain, w_query, w_key, w_value, w_out, mlp_gain, w_gate, w_up, w_down):
    rows, cols = tokens.shape
    planes = lax.axis_size("hi")
    chips = lax.axis_size("tensor") // 2
    count = 2 * chips
    depth = w_query.shape[0]
    width = cols * count
    heads_w = w_query.shape[1] // 2
    units = w_gate.shape[1] // 4
    padded = -(-units // LANES) * LANES

    bf16 = jnp.bfloat16
    vmem = pl.BlockSpec(memory_space=pltpu.VMEM)
    blocks = pltpu.VMEM((3, count, rows, cols), bf16)
    share = pltpu.VMEM((rows, cols), bf16)
    chunk = rows // 2
    chunks = 2 * rows // chunk
    dma = pltpu.SemaphoreType.DMA
    return pl.pallas_call(
        functools.partial(layer_kernel, planes, chips),
        out_shape=jax.ShapeDtypeStruct((rows, cols), bf16),
        in_specs=[vmem] * 10,
        out_specs=vmem,
        scratch_shapes=[
            pltpu.VMEM((width, heads_w + HEAD_DIM), bf16),
            pltpu.VMEM((2 * planes, heads_w, depth), bf16),
            pltpu.VMEM((2, 2, depth, 2 * padded), bf16),
            pltpu.VMEM((width, 2 * padded), bf16),
            pltpu.VMEM((2, depth, 2 * padded), bf16),
            pltpu.VMEM((2 * planes, padded, depth), bf16),
            pltpu.VMEM((2, units, depth), bf16),
            pltpu.VMEM((2 * rows, width), bf16),
            pltpu.VMEM((2, 2 * rows, width), bf16),
            pltpu.VMEM((chunk, width), bf16),
            pltpu.VMEM((2 * rows, heads_w), bf16),
            pltpu.VMEM((2, 4 * rows, HEAD_DIM), bf16),
            pltpu.VMEM((2 * rows, heads_w), bf16),
            pltpu.VMEM((4 * rows, padded), bf16),
            blocks, blocks, blocks, blocks,
            share, share,
            pltpu.VMEM((2, rows, cols), bf16),
            dma((3,)), dma((3,)),
            dma((2, planes, 2, 2)), dma((planes, 2, 2)),
            dma((2, 2)), dma((2, 2)),
            dma((planes, 2, 2)), dma((planes, 2, 2)),
            dma((5, 2)), dma((2, 2)),
            dma((3, count, 2)), dma((3, count, 2)), dma((3, count, 2)), dma((3, count, 2)),
            dma((3, chunks)), dma((3, chunks)),
            dma((2, 2)), dma((2, 2)),
            dma((3, count, 2)), dma((3, count, 2)), dma((3, count, 2)), dma((3, count, 2)),
        ],
        compiler_params=pltpu.CompilerParams(
            collective_id=1, has_side_effects=True, vmem_limit_bytes=66_000_000
        ),
    )(
        tokens, attn_gain.reshape(1, -1), mlp_gain.reshape(1, -1),
        w_query, w_key, w_value, w_out, w_gate, w_up, w_down,
    )


def solution(mesh):
    sizes = mesh.shape
    split = Mesh(
        mesh.devices.reshape(sizes["seq"] // 2, 2, sizes["tensor"]), ("hi", "pair", "tensor")
    )
    seq = ("hi", "pair")
    in_specs = (
        P(seq, "tensor"),
        P(),
        P(seq, "tensor"),
        P(seq, "tensor"),
        P(seq, "tensor"),
        P("tensor", seq),
        P(),
        P(seq, "tensor"),
        P(seq, "tensor"),
        P("tensor", seq),
    )
    return jax.shard_map(
        per_device, mesh=split, in_specs=in_specs, out_specs=P(seq, "tensor"), check_vma=False
    )
```

time: 241 us -> 202 us (0.84)
  Pallas kernels: 222 us -> 197 us
  local copies, waits for them, and re-layouts: 13.3 us -> 1.87 us
  other arithmetic: 3.54 us -> 0 us
    pallas_call x1, Pallas kernels: 222 us -> 197 us  [per_device(): pl.pallas_call(functools.partial(layer_kernel, planes, chips), out_shape=...]
    unnamed x31 -> x1, local copies, waits for them, and re-layouts: 8.02 us -> 1.87 us
    another operation x5 -> x0, other arithmetic: 2.76 us -> none  [the longest x3 1.78 us: per_device(): mlp_w = jnp.stack(mlp_w).reshape(2, 2, depth, 3 * padded)]
    another operation x3 -> x0, local copies, waits for them, and re-layouts: 2.52 us -> none  [the longest x1 2.51 us: per_device(): mlp_w = jnp.stack(mlp_w).reshape(2, 2, depth, 3 * padded)]
where the time goes in v2:
time: 202 us; the launch traced here: 199 us
  Pallas kernels  197 us (98%)
    pallas_call x1, Pallas kernels, per_device(): pl.pallas_call(functools.partial(layer_kernel, planes, chips), out_shape=...  197 us

profile of v2, /device:TPU:0, one launch (start us, length us, event | category | flops | bytes accessed | tf_op | source)
XLA Modules:
  0.0 198.9 jit_solution(4078332587329502634)
XLA Ops:
  0.0 197.0 %shard_map.100 = bf16[512,512]{1,0:T(8,128)(2,1)} custom-call(bf16[512,512]{1,0:T(8,128)(2,1)} %x_ref.1, f32[1,2048]{1,0:T(1,128)} %bitcast.2, f32[1,2048]{1,0:T(1,128)} %bitcast.3, bf16[256,512]{1,0:T(8,128)(2,1)} %wq.1, bf16[256,128]{1,0:T(8,128)(2,1)} %wk.1, bf16[256,128]{1,0:T(8,128)(2,1)} %wv.1, bf16[512,256]{1,0:T(8,128)(2,1)} %wo.1, ...), custom_call_target="tpu_custom_call" | custom-call | tf_op jit(solution)/shard_map/pallas_call | solution.py:623
  197.0 1.9 copy.12

commit v3 on v2

--- a/solution.py
+++ b/solution.py
@@ -20,7 +20,7 @@
 
 def layer_kernel(
     planes, chips, x_ref, gain1, gain2, wq, wk, wv, wo, wg, wu, wd, out_ref,
-    qkv_full, wo_full, gu_own, gu_full, gu_trade, wd_full, wd_trade, held1, held2, nbuf, qbuf, kv, att, hidden,
+    qkv_full, wo_full, gu_own, gu_full, gu_trade, wd_full, wd_trade, held1, held2, nbuf, qbuf, kv, hidden,
     given, near, stage, far, stream, leave, arrive,
     at_s, at_r, az_s, az_r, mt_s, mt_r, mz_s, mz_r, loc, kept,
     g_s, g_r, gp_s, gp_r, kv_s, kv_r, zx_s, zx_r, rn_s, rn_r, rf_s, rf_r,
@@ -30,7 +30,7 @@
     depth = wq.shape[0]
     heads_w = qbuf.shape[1]
     units, padded = wd.shape[0] // 4, hidden.shape[1]
-    gu_w = 2 * padded
+    aligned = depth % LANES == 0
     count = 2 * chips
     h, p, t = lax.axis_index("hi"), lax.axis_index("pair"), lax.axis_index("tensor")
     core = lax.rem(t, 2)
@@ -162,8 +162,8 @@
             copy = sent(place, place, az_s.at[way, k, j, part], az_r.at[src, j, part], dev(h, p, t))
             pl.when(cond)(lambda copy=copy: copy.wait_recv())
 
-    def a_relay(k, part):
-        for way in range(2):
+    def a_relay(k, part, ways=(0, 1)):
+        for way in ways:
             a_wait(k, part, way, False)
             for j in range(2):
                 a_send(k, j, part, ways=(way,))
@@ -219,6 +219,9 @@
     def m_slice(src, j, part):
         if part:
             return wd_full.at[src * 2 + j, pl.ds(0, units), :]
+        if aligned:
+            lanes = pl.ds(pl.multiple_of((src * 2 + j) * depth, depth), depth)
+            return gu_full.at[:, pl.ds(0, units), lanes]
         return gu_full.at[at_rows(src, j), :]
 
     def m_source(traded, g, part):
@@ -243,17 +246,17 @@
             m_source(traded, parity, part), m_slice(h, j, part), kept.at[int(traded), part]
         )
 
-    def m_up(traded, part, also=True):
-        for d in range(planes - 1, 0, -1):
+    def m_up(traded, part, also=True, steps=None):
+        for d in steps or range(planes - 1, 0, -1):
             m_send(h + d, (h + d < planes) & also, traded, part)
 
-    def m_down(traded, part, also=True):
-        for d in range(planes - 1, 0, -1):
+    def m_down(traded, part, also=True, steps=None):
+        for d in steps or range(planes - 1, 0, -1):
             m_send(h - d, (h - d >= 0) & also, traded, part)
 
-    def m_outward(traded, part):
-        m_up(traded, part, parity == 1)
-        m_down(traded, part, parity == 0)
+    def m_outward(traded, part, steps=None):
+        m_up(traded, part, parity == 1, steps)
+        m_down(traded, part, parity == 0, steps)
 
     def m_inward(traded, part):
         m_up(traded, part, parity == 0)
@@ -271,13 +274,38 @@
                 ).wait_recv()
 
     def pack():
-        zeros = jnp.zeros((depth, padded - units), gu_own.dtype)
-        for b in range(4):
-            lanes = slice(b * units, (b + 1) * units)
-            for n, ref in enumerate((wg, wu)):
-                gu_own[b // 2, b % 2, :, n * padded : (n + 1) * padded] = jnp.concatenate(
-                    [ref[:, lanes], zeros], axis=1
-                )
+        for n, ref in enumerate((wg, wu)):
+            turned = ref[...].T if aligned else ref[...]
+            for b in range(4):
+                cut = slice(b * units, (b + 1) * units)
+                if aligned:
+                    gu_own[b // 2, b % 2, n] = turned[cut]
+                else:
+                    gu_own[b // 2, b % 2, :, n * padded : (n + 1) * padded] = jnp.pad(
+                        turned[:, cut], ((0, 0), (0, padded - units))
+                    )
+        if aligned:
+            gu_full[:, units:, :] = jnp.zeros((2, padded - units, gu_full.shape[2]), gu_full.dtype)
+
+    def gate_up(left):
+        if aligned:
+            return product_t(left, gu_full[...].reshape(2 * padded, gu_full.shape[2]))
+        return jnp.dot(left, gu_full[...], preferred_element_type=jnp.float32)
+
+    step = 32
+
+    def norm_half(hold, gain, i, put):
+        @pl.loop(0, 2 * half // step)
+        def _(index):
+            run, at = lax.div(index, half // step), lax.rem(index, half // step)
+            source = pl.ds(pl.multiple_of(run * rows + i * half + at * step, step), step)
+            target = source
+            if put is None:
+                target = pl.ds(pl.multiple_of(index * step, step), step)
+            values = hold[source, :].astype(jnp.float32)
+            mean_square = jnp.mean(values * values, axis=1, keepdims=True)
+            scaled = values * lax.rsqrt(mean_square + 1e-06) * gain[...]
+            nbuf[target, :] = scaled.astype(nbuf.dtype)
 
     mark("start")
     qkv_trade()
@@ -314,21 +342,11 @@
     go(mtrade(0, 0))
     for i in range(2):
         gather_rest(0, i, x_ref, held1)
+        norm_half(held1, gain1, i, 0)
     mark("a_wait")
     a_finish(0)
 
-    step = 32
-    chunk = nbuf.shape[0]
-
-    def norm_chunk(hold, start, size, gain):
-        @pl.loop(0, size // step)
-        def _(index):
-            source = pl.ds(pl.multiple_of(start + index * step, step), step)
-            values = hold[source, :].astype(jnp.float32)
-            mean_square = jnp.mean(values * values, axis=1, keepdims=True)
-            scaled = values * lax.rsqrt(mean_square + 1e-06) * gain[...]
-            nbuf[pl.ds(pl.multiple_of(index * step, step), step), :] = scaled.astype(nbuf.dtype)
-
+    chunk = rows // 2
     scale = HEAD_DIM ** (-0.5) * LOG2E
     chunks = 2 * rows // chunk
 
@@ -348,9 +366,8 @@
     mark("qkv")
     for i in range(chunks):
         if i == 1:
-            a_relay(1, 1)
-        norm_chunk(held1, i * chunk, chunk, gain1)
-        made = jnp.dot(nbuf[...], qkv_full[...], preferred_element_type=jnp.float32)
+            a_relay(1, 1, ways=(1,))
+        made = jnp.dot(nbuf[i * chunk : (i + 1) * chunk, :], qkv_full[...], preferred_element_type=jnp.float32)
         qbuf[i * chunk : (i + 1) * chunk, :] = (made[:, :heads_w] * scale).astype(qbuf.dtype)
         kv[p, 2 * rows + i * chunk : 2 * rows + (i + 1) * chunk, :] = made[:, heads_w:].astype(
             kv.dtype
@@ -359,10 +376,9 @@
         go(kv_across(p, 1, i))
 
     mark("wo_relay")
+    a_relay(1, 1, ways=(0,))
     for k in range(2, planes - 1):
         a_relay(k, 1)
-    m_down(False, 0)
-    m_up(False, 0)
 
     mark("kv_wait")
     for i in range(chunks):
@@ -372,6 +388,7 @@
         kv_across(other, 1, i).wait_recv()
         pl.when(h > 0)(lambda i=i: kv_across(other, 0, i).wait_recv())
     go(mtrade(1, 0))
+    m_down(False, 0)
     mark("attention")
     qrows = 256
     edge = WINDOW
@@ -418,7 +435,7 @@
             mixed += jnp.dot(
                 e2.astype(jnp.bfloat16), span(1, edge, qrows), preferred_element_type=jnp.float32
             )
-            att[pl.ds(base, qrows), lanes] = (mixed / total).astype(att.dtype)
+            qbuf[pl.ds(base, qrows), lanes] = (mixed / total).astype(qbuf.dtype)
 
     nt = 64
 
@@ -432,58 +449,75 @@
         ]
         return jnp.concatenate(made, axis=1)
 
+    given_sends = {}
+
     def give(n, k, left, first, width, right):
+        slot = n % 2
         for i in range(2):
+            before = given_sends.pop((slot, id(k), i), None)
+            if before is not None:
+                before()
+                finish[:] = [wait for wait in finish if wait is not before]
             value = term(left, first, width, right, ahead(k, sib), i)
-            given[n, k, halves[i], :] = value.astype(given.dtype)
+            given[slot, k, halves[i], :] = value.astype(given.dtype)
             go(
                 sent(
-                    given.at[n, k, halves[i]], near.at[n, k, halves[i]],
+                    given.at[slot, k, halves[i]], near.at[n, k, halves[i]],
                     rn_s.at[n, k, i], rn_r.at[n, k, i], dev(h, p, sib),
                 )
             )
+            given_sends[slot, id(k), i] = finish[-1]
 
     def own(n, k, i, extra, left, first, width, right):
         came = near.at[n, k, halves[i]]
         sent(came, came, rn_s.at[n, k, i], rn_r.at[n, k, i], dev(h, p, sib)).wait_recv()
         value = term(left, first, width, right, ahead(k, t), i)
         value = value + near[n, k, halves[i], :].astype(jnp.float32)
-        if extra:
-            landed(n, 3, i).wait_recv()
-            value = value + far[n, 3, halves[i], :].astype(jnp.float32)
+        if extra is not None:
+            landed(*extra, i).wait_recv()
+            value = value + far[extra[0], extra[1] - 1, halves[i], :].astype(jnp.float32)
         stage[n, k, halves[i], :] = value.astype(stage.dtype)
 
     def onward(n, k, slot, way, i):
         go(
             sent(
-                stage.at[n, k, halves[i]], far.at[n, slot, halves[i]],
+                stage.at[n, k, halves[i]], far.at[n, slot - 1, halves[i]],
                 rf_s.at[n, slot, i], rf_r.at[n, slot, i], dev(h, *ahead(way, t)),
             )
         )
 
-    def sums_far(n, *terms):
-        give(n, 3, *terms)
-        give(n, far_k, *terms)
+    def sums_far(n, over, *terms):
+        if over != "join":
+            give(n, 3, *terms)
+            give(n, far_k, *terms)
         for i in range(2):
-            own(n, 3, i, False, *terms)
-            onward(n, 3, 3, near_k, i)
+            own(n, 3, i, (1, 3) if over == "join" else None, *terms)
+            if over == "leave":
+                go(
+                    sent(
+                        stage.at[n, 3, halves[i]], far.at[n, 2, halves[i]],
+                        rf_s.at[n, 3, i], rf_r.at[n, 3, i], dev(partner, p, t),
+                    )
+                )
+            else:
+                onward(n, 3, 3, near_k, i)
 
     def sums_near(n, *terms):
         give(n, near_k, *terms)
         for i in range(2):
-            own(n, near_k, i, False, *terms)
+            own(n, near_k, i, None, *terms)
             onward(n, near_k, near_k, near_k, i)
 
-    def sums_last(n, *terms):
+    def sums_last(n, relayed, *terms):
         give(n, 0, *terms)
         for i in range(2):
-            own(n, far_k, i, True, *terms)
+            own(n, far_k, i, (n, 3) if relayed else None, *terms)
             onward(n, far_k, far_k, far_k, i)
         for i in range(2):
-            own(n, 0, i, False, *terms)
+            own(n, 0, i, None, *terms)
 
     def landed(n, k, i):
-        came = far.at[n, k, halves[i]]
+        came = far.at[n, k - 1, halves[i]]
         return sent(came, came, rf_s.at[n, k, i], rf_r.at[n, k, i], dev(h, p, t))
 
     def sums_end(n, i, extra, target):
@@ -495,26 +529,24 @@
             part = pl.ds(pl.multiple_of(i * half + index * nt, nt), nt)
             total = stage[n, 0, part, :].astype(jnp.float32)
             for k in (1, 2):
-                total = total + far[n, k, part, :].astype(jnp.float32)
+                total = total + far[n, k - 1, part, :].astype(jnp.float32)
             for ref in extra:
                 total = total + ref[part, :].astype(jnp.float32)
             target[part, :] = total.astype(target.dtype)
 
+    m_up(False, 0)
     mark("trade_wait")
     for g in range(2):
         mtrade_wait(g, 0)
     m_keep(True, 0).start()
     m_outward(True, 0)
-    m_outward(False, 1)
     mark("wo_wait")
     a_finish(1)
     mark("sums0")
     own_wo.wait()
-    sums_far(0, att, 0, heads_w, wo_full)
-    sums_near(0, att, 0, heads_w, wo_full)
-    sums_last(0, att, 0, heads_w, wo_full)
-    go(mtrade(0, 1))
-    go(mtrade(1, 1))
+    sums_far(0, None, qbuf, 0, heads_w, wo_full)
+    sums_near(0, qbuf, 0, heads_w, wo_full)
+    sums_last(0, True, qbuf, 0, heads_w, wo_full)
     mark("end0")
     gives = []
     for i in range(2):
@@ -529,58 +561,63 @@
         gather_start(1, i, stream, held2.at[0])
     mark("send2")
     m_inward(True, 0)
+    m_outward(False, 1)
     m_inward(False, 1)
-    for g in range(2):
-        mtrade_wait(g, 1)
-    m_keep(True, 1).start()
-    m_outward(True, 1)
-    m_inward(True, 1)
     mark("zwait")
     gather_relay(1, held2.at[0])
+    go(mtrade(0, 1))
+    go(mtrade(1, 1))
     mark("gather2a")
     for i in range(2):
         gives[i].wait_recv()
         gather_start(2, i, arrive.at[0], held2.at[1])
     for i in range(2):
         gather_rest(1, i, stream, held2.at[0])
+        norm_half(held2.at[0], gain2, i, 0)
+    mark("wd_trade")
+    for g in range(2):
+        mtrade_wait(g, 1)
+    m_keep(True, 1).start()
+    m_outward(True, 1)
+    m_inward(True, 1)
     mark("relay2b")
     gather_relay(2, held2.at[1])
     mark("gu_wait")
     m_wait(0)
 
 
-    def mlp_half(plane, i):
-        for run in range(2):
-            start = run * rows + i * half
-            norm_chunk(held2.at[plane], start, half, gain2)
-            made = jnp.dot(nbuf[0:half, :], gu_full[...], preferred_element_type=jnp.float32)
-            gate, up = made[:, :padded], made[:, padded:]
-            value = gate / (1.0 + jnp.exp(-gate)) * up
-            start = plane * 2 * rows + start
-            hidden[start : start + half, :] = value.astype(hidden.dtype)
+    def mlp_rows(start, put):
+        made = gate_up(nbuf[put : put + rows, :])
+        gate, up = made[:, :padded], made[:, padded:]
+        value = (gate / (1.0 + jnp.exp(-gate)) * up).astype(hidden.dtype)
+        for at, size, first in start:
+            hidden[at : at + size, :] = value[first : first + size]
 
     mark("mlp0")
-    for i in range(2):
-        mlp_half(0, i)
+    for run in range(2):
+        mlp_rows(((run * rows, rows, 0),), run * rows)
     for i in range(2):
         mark("gather2b")
         gather_rest(2, i, arrive.at[0], held2.at[1])
         mark("mlp1")
-        mlp_half(1, i)
+        norm_half(held2.at[1], gain2, i, None)
+        first = 2 * rows + i * half
+        mlp_rows(((first, half, 0), (first + rows, half, half)), 0)
     mark("wd_wait")
     m_wait(1)
 
     mark("sums1")
-    theirs = (1, hidden, 2 * rows, padded, wd_full)
-    ours = (2, hidden, 0, padded, wd_full)
-    sums_far(*theirs)
-    sums_near(*theirs)
-    sums_far(*ours)
+    theirs = (hidden, 2 * rows, padded, wd_full)
+    ours = (hidden, 0, padded, wd_full)
+    sums_far(1, "leave", *theirs)
+    sums_near(1, *theirs)
     mark("sums2")
-    sums_last(*theirs)
-    sums_near(*ours)
+    sums_last(1, False, *theirs)
+    for k in (3, far_k):
+        give(2, k, *ours)
     mark("sums3")
-    sums_last(*ours)
+    sums_far(2, "join", *ours)
+    sums_near(2, *ours)
     mark("end1")
     backs = []
     for i in range(2):
@@ -592,6 +629,8 @@
             )
         )
         go(backs[i])
+    mark("sums4")
+    sums_last(2, True, *ours)
     mark("end2")
     for i in range(2):
         backs[i].wait_recv()
@@ -613,6 +652,9 @@
     units = w_gate.shape[1] // 4
     padded = -(-units // LANES) * LANES
 
+    piece, gathered = (2, units, depth), (2, padded, width)
+    if depth % LANES:
+        piece, gathered = (depth, 2 * padded), (width, 2 * padded)
     bf16 = jnp.bfloat16
     vmem = pl.BlockSpec(memory_space=pltpu.VMEM)
     blocks = pltpu.VMEM((3, count, rows, cols), bf16)
@@ -628,19 +670,19 @@
         scratch_shapes=[
             pltpu.VMEM((width, heads_w + HEAD_DIM), bf16),
             pltpu.VMEM((2 * planes, heads_w, depth), bf16),
-            pltpu.VMEM((2, 2, depth, 2 * padded), bf16),
-            pltpu.VMEM((width, 2 * padded), bf16),
-            pltpu.VMEM((2, depth, 2 * padded), bf16),
+            pltpu.VMEM((2, 2, *piece), bf16),
+            pltpu.VMEM(gathered, bf16),
+            pltpu.VMEM((2, *piece), bf16),
             pltpu.VMEM((2 * planes, padded, depth), bf16),
             pltpu.VMEM((2, units, depth), bf16),
             pltpu.VMEM((2 * rows, width), bf16),
             pltpu.VMEM((2, 2 * rows, width), bf16),
-            pltpu.VMEM((chunk, width), bf16),
+            pltpu.VMEM((2 * rows, width), bf16),
             pltpu.VMEM((2 * rows, heads_w), bf16),
             pltpu.VMEM((2, 4 * rows, HEAD_DIM), bf16),
-            pltpu.VMEM((2 * rows, heads_w), bf16),
             pltpu.VMEM((4 * rows, padded), bf16),
-            blocks, blocks, blocks, blocks,
+            pltpu.VMEM((2, count, rows, cols), bf16), blocks, blocks,
+            pltpu.VMEM((3, count - 1, rows, cols), bf16),
             share, share,
             pltpu.VMEM((2, rows, cols), bf16),
             dma((3,)), dma((3,)),
@@ -654,7 +696,7 @@
             dma((3, count, 2)), dma((3, count, 2)), dma((3, count, 2)), dma((3, count, 2)),
         ],
         compiler_params=pltpu.CompilerParams(
-            collective_id=1, has_side_effects=True, vmem_limit_bytes=66_000_000
+            collective_id=1, has_side_effects=True, vmem_limit_bytes=66_900_000
         ),
     )(
         tokens, attn_gain.reshape(1, -1), mlp_gain.reshape(1, -1),

time: 202 us -> 184 us (0.911); the launches traced: 199 us -> 184 us
  Pallas kernels: 197 us -> 182 us
    pallas_call x1, Pallas kernels: 197 us -> 182 us  [per_device(): pl.pallas_call(functools.partial(layer_kernel, planes, chips), out_shape=...]
where the time goes in v3:
time: 184 us
  Pallas kernels  182 us (99%)
  local copies, waits for them, and re-layouts  1.87 us (1%)
    pallas_call x1, Pallas kernels, per_device(): pl.pallas_call(functools.partial(layer_kernel, planes, chips), out_shape=...  182 us

profile of v3, /device:TPU:0, one launch (start us, length us, event | category | flops | bytes accessed | tf_op | source)
XLA Modules:
  0.0 183.9 jit_solution(3242911115842675793)
XLA Ops:
  0.0 182.0 %shard_map.100 = bf16[512,512]{1,0:T(8,128)(2,1)} custom-call(bf16[512,512]{1,0:T(8,128)(2,1)} %x_ref.1, f32[1,2048]{1,0:T(1,128)} %bitcast.2, f32[1,2048]{1,0:T(1,128)} %bitcast.3, bf16[256,512]{1,0:T(8,128)(2,1)} %wq.1, bf16[256,128]{1,0:T(8,128)(2,1)} %wk.1, bf16[256,128]{1,0:T(8,128)(2,1)} %wv.1, bf16[512,256]{1,0:T(8,128)(2,1)} %wo.1, ...), custom_call_target="tpu_custom_call" | custom-call | tf_op jit(solution)/shard_map/pallas_call | solution.py:665
  182.0 1.9 %copy.12 = bf16[512,512]{1,0:T(8,128)(2,1)} copy(bf16[512,512]{1,0:T(8,128)(2,1)} %shard_map.100) | data formatting | bytes 1048576
